TPU v7x, 128 devices: a whole 4x4x4 slice. The times are simulated.
128 devices in a mesh: right: 64 (over z, y, x), left: 2 (over core).
Axes of the slice: x: 4, y: 4, z: 4, core: 2. Of those that a mesh axis runs over, the one named last changes fastest.
Arguments:
- psi_init: float32 [1536, 2, 2, 1536], P('left', None, None, 'right')
- env_left: float32 [1536, 8, 1536], P('left')
- env_right: float32 [1536, 8, 1536], P('right')
- mpo_pair: float32 [8, 8, 2, 2, 2, 2], replicated
Outputs:
- output 1: float32 [5], replicated
- output 2: float32 [5], replicated
- output 3: float32 [1536, 2, 2, 1536], P('left', None, None, 'right')
All inputs are finite; a program needn't handle non-finite values.
Results may differ from a plain program's by a relative error of at most 0.001.
Values sent between devices are 32-bit elements.
A program may use at most 1 GiB of HBM per device.

v0:
```python
import math
import jax
import jax.numpy as jnp
from jax import lax
from jax.sharding import PartitionSpec as P

KRYLOV_STEPS = 5
PREC_MODE = lax.Precision.HIGHEST
BOTH_AXES = ("right", "left")


def project_out(krylov_basis, residual, coeffs):
    for vec_idx, basis_vec in enumerate(krylov_basis):
        residual = residual - coeffs[vec_idx] * basis_vec
    return residual


def global_dots(krylov_basis, residual):
    local_dots = jnp.stack([jnp.sum(basis_vec * residual) for basis_vec in krylov_basis])
    return lax.psum(local_dots, BOTH_AXES)


def solution(mesh):
    n_devices = mesh.shape["left"] * mesh.shape["right"]
    psi_spec = P("left", None, None, "right")

    def local_fn(psi_loc, env_left, env_right, mpo_pair):
        left_full = lax.all_to_all(env_left, "left", 2, 0, tiled=True)

        def apply_ham(in_vec):
            vec_full = lax.all_gather(in_vec, "left", axis=0, tiled=True)
            stage_one = jnp.einsum("alc,asub->lcsub", left_full, vec_full, precision=PREC_MODE, preferred_element_type=jnp.float32)
            stage_two = jnp.einsum("lrsutv,lcsub->rtvcb", mpo_pair, stage_one, precision=PREC_MODE, preferred_element_type=jnp.float32)
            part_out = jnp.einsum("rtvcb,bre->tvce", stage_two, env_right, precision=PREC_MODE, preferred_element_type=jnp.float32)
            reduced = lax.psum_scatter(part_out, "right", scatter_dimension=3, tiled=True)
            return jnp.transpose(reduced, (2, 0, 1, 3))

        init_norm = jnp.sqrt(lax.psum(jnp.sum(psi_loc * psi_loc), BOTH_AXES))
        krylov_basis = [psi_loc / init_norm]
        alpha_list = []
        beta_list = []
        for step_idx in range(KRYLOV_STEPS):
            residual = apply_ham(krylov_basis[-1])
            first_pass = global_dots(krylov_basis, residual)
            alpha_list.append(first_pass[-1])
            residual = project_out(krylov_basis, residual, first_pass)
            second_pass = global_dots(krylov_basis, residual)
            residual = project_out(krylov_basis, residual, second_pass)
            beta_val = jnp.sqrt(lax.psum(jnp.sum(residual * residual), BOTH_AXES))
            beta_list.append(beta_val)
            krylov_basis.append(residual / beta_val)
        out_scale = math.sqrt(float(psi_loc.size * n_devices))
        return jnp.stack(alpha_list), jnp.stack(beta_list), krylov_basis[-1] * out_scale

    lanczos_run = jax.shard_map(
        local_fn,
        mesh=mesh,
        in_specs=(psi_spec, P("left", None, None), P("right", None, None), P()),
        out_specs=(P(), P(), psi_spec),
        check_vma=False,
    )
    return lanczos_run
```

profile of v0, /device:TPU:1, one launch (start us, length us, event | category | flops | bytes accessed | tf_op | source)
XLA Modules:
  0.0 2668.6 jit_solution(17019246935834099309)
XLA Ops:
  8.9 37.1 %copy.44 = f32[768,8,1536]{0,1,2:T(8,128)} copy(f32[768,8,1536]{2,1,0:T(8,128)} %param.5) | data formatting | bytes 75497472 | tf_op args[1]
  46.0 15.9 all-to-all-start
  61.9 87.7 %psum.112 = f32[]{:T(128)} all-reduce(f32[]{:T(128)} %multiply_reduce_fusion.20), channel_id=1, replica_groups=mesh['right'=64,'left'=2] {'right','left'}, use_global_device_ids=true, to_apply=%region_1.0 | all-reduce | flops 1 | bytes 8 | tf_op jit(solution)/shard_map/psum | solution.py:38
  153.1 37.0 %copy.94 = f32[2,768,8,768]{3,1,0,2:T(8,128)} copy(f32[2,768,8,768]{1,2,3,0:T(8,128)} %bitcast.4) | data formatting | bytes 75497472 | tf_op jit(solution)/shard_map/all_to_all | solution.py:28
  190.1 26.0 convolution_bitcast_fusion.9
  219.1 16.1 convolution_bitcast_fusion.4
  235.2 6.7 copy.51
  241.9 234.1 %reduce-scatter.6.cloned.1.call-done = f32[2,2,768,24]{2,3,1,0:T(8,128)} async-done(((f32[2,2,768,1536]{2,3,1,0:T(8,128)}), f32[2,2,768,24]{2,3,1,0:T(8,128)}) %reduce-scatter.6.cloned.1.call-update) | async-done | bytes 294928 | tf_op jit(solution)/shard_map/reduce_scatter | solution.py:35
  477.7 64.5 %psum.113 = f32[1]{0:T(128)} all-reduce(f32[1]{0:T(128)} %bitcast.19), channel_id=1, replica_groups=mesh['right'=64,'left'=2] {'right','left'}, use_global_device_ids=true, to_apply=%region_4.0 | all-reduce | flops 1 | bytes 8 | tf_op jit(solution)/shard_map/psum | solution.py:20
  544.4 62.5 %psum.114 = f32[]{:T(128)} all-reduce(f32[]{:T(128)} %multiply_reduce_fusion.19), channel_id=1, replica_groups=mesh['right'=64,'left'=2] {'right','left'}, use_global_device_ids=true, to_apply=%region_6.0 | all-reduce | flops 1 | bytes 8 | tf_op jit(solution)/shard_map/psum | solution.py:20
  609.9 64.1 %psum.115 = f32[]{:T(128)} all-reduce(f32[]{:T(128)} %multiply_reduce_fusion.18), channel_id=1, replica_groups=mesh['right'=64,'left'=2] {'right','left'}, use_global_device_ids=true, to_apply=%region_8.0 | all-reduce | flops 1 | bytes 8 | tf_op jit(solution)/shard_map/psum | solution.py:49
  680.0 26.0 convolution_bitcast_fusion.8
  708.9 16.1 convolution_bitcast_fusion.3
  725.0 6.7 copy.56
  731.8 233.7 %reduce-scatter.8.cloned.1.call-done = f32[2,2,768,24]{2,3,1,0:T(8,128)} async-done(((f32[2,2,768,1536]{2,3,1,0:T(8,128)}), f32[2,2,768,24]{2,3,1,0:T(8,128)}) %reduce-scatter.8.cloned.1.call-update) | async-done | bytes 294928 | tf_op jit(solution)/shard_map/reduce_scatter | solution.py:35
  968.5 64.4 %psum.116 = f32[2]{0:T(128)S(1)} all-reduce(f32[2]{0:T(128)S(1)} %pad_maximum_fusion), channel_id=1, replica_groups=mesh['right'=64,'left'=2] {'right','left'}, use_global_device_ids=true, to_apply=%region_12.0 | all-reduce | flops 2 | bytes 16 | tf_op jit(solution)/shard_map/psum | solution.py:20
  1037.7 62.4 %psum.117 = f32[2]{0:T(128)S(1)} all-reduce(f32[2]{0:T(128)S(1)} %pad_maximum_fusion.1), channel_id=1, replica_groups=mesh['right'=64,'left'=2] {'right','left'}, use_global_device_ids=true, to_apply=%region_15.0 | all-reduce | flops 2 | bytes 16 | tf_op jit(solution)/shard_map/psum | solution.py:20
  1100.7 4.2 multiply_reduce_fusion.15
  1104.9 64.1 %psum.118 = f32[]{:T(128)} all-reduce(f32[]{:T(128)} %get-tuple-element.40), channel_id=1, replica_groups=mesh['right'=64,'left'=2] {'right','left'}, use_global_device_ids=true, to_apply=%region_17.0 | all-reduce | flops 1 | bytes 8 | tf_op jit(solution)/shard_map/psum | solution.py:49
  1172.7 26.0 convolution_bitcast_fusion.7
  1201.6 16.1 convolution_bitcast_fusion.2
  1217.7 6.7 copy.61
  1224.4 233.8 %reduce-scatter.10.cloned.1.call-done = f32[2,2,768,24]{2,3,1,0:T(8,128)} async-done(((f32[2,2,768,1536]{2,3,1,0:T(8,128)}), f32[2,2,768,24]{2,3,1,0:T(8,128)}) %reduce-scatter.10.cloned.1.call-update) | async-done | bytes 294928 | tf_op jit(solution)/shard_map/reduce_scatter | solution.py:35
  1461.8 64.4 %psum.119 = f32[3]{0:T(128)S(1)} all-reduce(f32[3]{0:T(128)S(1)} %pad_maximum_fusion.2), channel_id=1, replica_groups=mesh['right'=64,'left'=2] {'right','left'}, use_global_device_ids=true, to_apply=%region_22.0 | all-reduce | flops 3 | bytes 24 | tf_op jit(solution)/shard_map/psum | solution.py:20
  1526.8 3.6 multiply_reduce_fusion.14
  1532.2 62.4 %psum.120 = f32[3]{0:T(128)S(1)} all-reduce(f32[3]{0:T(128)S(1)} %pad_maximum_fusion.3), channel_id=1, replica_groups=mesh['right'=64,'left'=2] {'right','left'}, use_global_device_ids=true, to_apply=%region_26.0 | all-reduce | flops 3 | bytes 24 | tf_op jit(solution)/shard_map/psum | solution.py:20
  1597.8 64.1 %psum.121 = f32[]{:T(128)} all-reduce(f32[]{:T(128)} %get-tuple-element.37), channel_id=1, replica_groups=mesh['right'=64,'left'=2] {'right','left'}, use_global_device_ids=true, to_apply=%region_28.0 | all-reduce | flops 1 | bytes 8 | tf_op jit(solution)/shard_map/psum | solution.py:49
  1665.6 26.1 convolution_bitcast_fusion.6
  1694.6 16.1 convolution_bitcast_fusion.1
  1710.7 6.7 copy.66
  1717.4 233.9 %reduce-scatter.12.cloned.1.call-done = f32[2,2,768,24]{2,3,1,0:T(8,128)} async-done(((f32[2,2,768,1536]{2,3,1,0:T(8,128)}), f32[2,2,768,24]{2,3,1,0:T(8,128)}) %reduce-scatter.12.cloned.1.call-update) | async-done | bytes 294928 | tf_op jit(solution)/shard_map/reduce_scatter | solution.py:35
  1955.6 64.4 %psum.122 = f32[4]{0:T(128)S(1)} all-reduce(f32[4]{0:T(128)S(1)} %pad_maximum_fusion.4), channel_id=1, replica_groups=mesh['right'=64,'left'=2] {'right','left'}, use_global_device_ids=true, to_apply=%region_34.0 | all-reduce | flops 4 | bytes 32 | tf_op jit(solution)/shard_map/psum | solution.py:20
  2020.6 4.3 multiply_reduce_fusion.10
  2027.5 62.4 %psum.123 = f32[4]{0:T(128)S(1)} all-reduce(f32[4]{0:T(128)S(1)} %pad_maximum_fusion.5), channel_id=1, replica_groups=mesh['right'=64,'left'=2] {'right','left'}, use_global_device_ids=true, to_apply=%region_39.0 | all-reduce | flops 4 | bytes 32 | tf_op jit(solution)/shard_map/psum | solution.py:20
  2090.5 3.2 multiply_reduce_fusion.6
  2093.7 64.1 %psum.124 = f32[]{:T(128)} all-reduce(f32[]{:T(128)} %get-tuple-element.34), channel_id=1, replica_groups=mesh['right'=64,'left'=2] {'right','left'}, use_global_device_ids=true, to_apply=%region_41.0 | all-reduce | flops 1 | bytes 8 | tf_op jit(solution)/shard_map/psum | solution.py:49
  2161.5 26.1 convolution_bitcast_fusion.5
  2190.4 15.9 convolution_bitcast_fusion
  2206.4 6.8 copy.71
  2213.2 233.6 %reduce-scatter.14.cloned.1.call-done = f32[2,2,768,24]{2,3,1,0:T(8,128)} async-done(((f32[2,2,768,1536]{2,3,1,0:T(8,128)}), f32[2,2,768,24]{2,3,1,0:T(8,128)}) %reduce-scatter.14.cloned.1.call-update) | async-done | bytes 294928 | tf_op jit(solution)/shard_map/reduce_scatter | solution.py:35
  2448.6 3.2 stack.166
  2451.8 64.4 %psum.125 = f32[5]{0:T(128)S(1)} all-reduce(f32[5]{0:T(128)S(1)} %stack.166), channel_id=1, replica_groups=mesh['right'=64,'left'=2] {'right','left'}, use_global_device_ids=true, to_apply=%region_48.0 | all-reduce | flops 5 | bytes 40 | tf_op jit(solution)/shard_map/psum | solution.py:20
  2516.9 5.0 multiply_reduce_fusion.1
  2521.9 3.3 stack.177
  2525.2 3.6 stack.167
  2528.8 62.4 %psum.126 = f32[5]{0:T(128)S(1)} all-reduce(f32[5]{0:T(128)S(1)} %stack.177), channel_id=1, replica_groups=mesh['right'=64,'left'=2] {'right','left'}, use_global_device_ids=true, to_apply=%region_54.0 | all-reduce | flops 5 | bytes 40 | tf_op jit(solution)/shard_map/psum | solution.py:20
  2591.9 3.8 multiply_reduce_fusion
  2595.7 64.1 %psum.127 = f32[]{:T(128)} all-reduce(f32[]{:T(128)} %get-tuple-element.31), channel_id=1, replica_groups=mesh['right'=64,'left'=2] {'right','left'}, use_global_device_ids=true, to_apply=%region_56.0 | all-reduce | flops 1 | bytes 8 | tf_op jit(solution)/shard_map/psum | solution.py:49
  (59 shorter events, 70.5 us)
Async XLA Ops:
  7.2 211.9 %copy-start = (f32[24,8,1536]{2,1,0:T(8,128)S(1)}, f32[24,8,1536]{2,1,0:T(8,128)}, u32[]{:S(2)}) copy-start(f32[24,8,1536]{2,1,0:T(8,128)} %param.6) | copy-start | bytes 3538948
  46.0 104.3 %copy-start.2 = (f32[8,8,2,2,2,2]{1,5,4,3,2,0:T(2,128)S(1)}, f32[8,8,2,2,2,2]{1,5,4,3,2,0:T(2,128)}, u32[]{:S(2)}) copy-start(f32[8,8,2,2,2,2]{1,5,4,3,2,0:T(2,128)} %param.7) | copy-start | bytes 12292
  46.0 104.4 %copy-start.1 = (f32[768,2,2,24]{0,3,2,1:T(8,128)S(1)}, f32[768,2,2,24]{0,3,2,1:T(8,128)}, u32[]{:S(2)}) copy-start(f32[768,2,2,24]{0,3,2,1:T(8,128)} %param.4) | copy-start | bytes 884740
  46.0 107.1 %all-to-all-start = ((f32[768,8,1536]{0,1,2:T(8,128)}), f32[768,8,1536]{0,1,2:T(8,128)}, u32[]{:S(2)}, u32[]{:S(2)}) async-start(f32[768,8,1536]{0,1,2:T(8,128)} %copy.44), calls=%async_computation | async-start | bytes 75497472 | tf_op jit(solution)/shard_map/all_to_all | solution.py:28
  61.9 414.1 %reduce-scatter.6.cloned.1.call-start = ((), (), s32[]{:S(2)}) async-start(), calls=%async_computation.6 | async-start | bytes 19169280 | tf_op jit(solution)/shard_map/reduce_scatter | solution.py:35
  241.9 723.6 %reduce-scatter.8.cloned.1.call-start = ((), (), s32[]{:S(2)}) async-start(), calls=%async_computation.7 | async-start | bytes 19169280 | tf_op jit(solution)/shard_map/reduce_scatter | solution.py:35
  731.7 726.6 %reduce-scatter.10.cloned.1.call-start = ((), (), s32[]{:S(2)}) async-start(), calls=%async_computation.8 | async-start | bytes 19169280 | tf_op jit(solution)/shard_map/reduce_scatter | solution.py:35
  1224.4 727.0 %reduce-scatter.12.cloned.1.call-start = ((), (), s32[]{:S(2)}) async-start(), calls=%async_computation.9 | async-start | bytes 19169280 | tf_op jit(solution)/shard_map/reduce_scatter | solution.py:35
  1717.4 729.4 %reduce-scatter.14.cloned.1.call-start = ((), (), s32[]{:S(2)}) async-start(), calls=%async_computation.10 | async-start | bytes 19169280 | tf_op jit(solution)/shard_map/reduce_scatter | solution.py:35
Sparse Core Ops, SparseCore 0:
  242.0 234.0 reduce-scatter.5
  731.8 233.6 reduce-scatter.7
  1224.5 233.7 reduce-scatter.9
  1717.5 233.8 reduce-scatter.11
  2213.3 233.4 reduce-scatter.13
where the time goes:
time: 2680 us; the launch traced here: 2670 us
  waiting for transfers between devices  1170 us (44%)
  blocking collectives  1060 us (40%)
  matrix products  225 us (8%)
  local copies, waits for them, and re-layouts  123 us (5%)
  other arithmetic  59.6 us (2%)
    reduce_scatter x5, waiting for transfers between devices, apply_ham(): lax.psum_scatter(part_out, 'right', scatter_dimension=3, tiled=True)  1170 us
    psum x10, blocking collectives, global_dots(): return lax.psum(local_dots, BOTH_AXES)  634 us
    psum x5, blocking collectives, local_fn(): beta_val = jnp.sqrt(lax.psum(jnp.sum(residual * residual), BOTH_AXES))  320 us
    dot_general x5, matrix products, apply_ham(): jnp.einsum('alc,asub->lcsub', left_full, vec_full, precision=PREC_MODE, p...  130 us
    psum x1, blocking collectives, local_fn(): init_norm = jnp.sqrt(lax.psum(jnp.sum(psi_loc * psi_loc), BOTH_AXES))  87.7 us
    dot_general x5, matrix products, apply_ham(): jnp.einsum('rtvcb,bre->tvce', stage_two, env_right, precision=PREC_MODE,...  80.4 us
  transfers between devices with their start and end apart: 6, of which 5 were waited for; matrix products, arithmetic and copies ran while one was open for 0% of the time, Pallas kernels for 0%

commit v1 on v0

v1 whole, which is shorter than its diff:
```python
import math
import jax
import jax.numpy as jnp
from jax import lax
from jax.sharding import Mesh
from jax.sharding import PartitionSpec as P

KRYLOV_STEPS = 5
PREC_MODE = lax.Precision.HIGHEST
ALL_AXES = ("z", "yb", "ya", "x", "core")
ROW_AXES = ("core", "ya", "x")
COL_AXES = ("z", "yb")


def solution(mesh):
    grid = Mesh(mesh.devices.reshape(4, 2, 2, 4, 2), ALL_AXES)
    n_devices = grid.devices.size
    psi_spec = P("core", None, None, ("z", "yb", "ya", "x"))

    def local_fn(psi_loc, env_left, env_right, mpo_pair):
        n_total = float(psi_loc.size * n_devices)
        rows_loc = psi_loc.shape[0] // 8
        row_idx = lax.axis_index(("ya", "x"))
        left_blk = lax.dynamic_slice_in_dim(env_left, row_idx * rows_loc, rows_loc, 0)
        right_blk = lax.all_gather(env_right, ("ya", "x"), axis=0, tiled=True)
        psi = lax.all_to_all(psi_loc, ("ya", "x"), 0, 3, tiled=True)
        psi = psi.reshape(psi.shape[0], 4, psi.shape[3])
        n_mpo = mpo_pair.shape[0]
        mix = mpo_pair.reshape(n_mpo, n_mpo, 4, 4)

        def apply_ham(vec):
            full = lax.all_gather(vec, ROW_AXES, axis=0, tiled=True)
            t1 = jnp.einsum("cla,asb->lcsb", left_blk, full, precision=PREC_MODE, preferred_element_type=jnp.float32)
            t2 = jnp.einsum("lrst,lcsb->ctrb", mix, t1, precision=PREC_MODE, preferred_element_type=jnp.float32)
            part = jnp.einsum("ctrb,bre->cte", t2, right_blk, precision=PREC_MODE, preferred_element_type=jnp.float32)
            return lax.psum_scatter(part, COL_AXES, scatter_dimension=2, tiled=True)

        def dots(basis, vec, extra=()):
            loc = [jnp.sum(b * vec) for b in basis] + [jnp.sum(p * q) for p, q in extra]
            return lax.psum(jnp.stack(loc), ALL_AXES)

        raw = apply_ham(psi)
        inv0 = 1.0 / jnp.sqrt(dots([psi], psi)[0])
        basis = [psi * inv0]
        images = [raw * inv0]
        gram = {}
        alphas, betas = [], []
        for step in range(KRYLOV_STEPS):
            cur = images[-1]
            if step + 1 < KRYLOV_STEPS:
                nxt = apply_ham(cur)
            k = step + 1
            red = dots(basis, cur, [(b, basis[-1]) for b in basis])
            c1 = red[:k]
            for i in range(k):
                gram[i, step] = gram[step, i] = red[k + i]
            alphas.append(c1[-1])
            res = cur
            for i in range(k):
                res = res - c1[i] * basis[i]
            red2 = dots(basis, res, [(res, res)])
            c2 = red2[:k]
            sq = red2[k]
            for i in range(k):
                sq = sq - 2.0 * c2[i] * c2[i]
            for i in range(k):
                for m in range(k):
                    sq = sq + c2[i] * c2[m] * gram[i, m]
                res = res - c2[i] * basis[i]
            beta = jnp.sqrt(sq)
            betas.append(beta)
            inv = 1.0 / beta
            basis.append(res * inv)
            if step + 1 < KRYLOV_STEPS:
                for i in range(k):
                    nxt = nxt - (c1[i] + c2[i]) * images[i]
                images.append(nxt * inv)
        out = basis[-1] * math.sqrt(n_total)
        out = out.reshape(out.shape[0], 2, 2, out.shape[2])
        out = lax.all_to_all(out, ("ya", "x"), 3, 0, tiled=True)
        return jnp.stack(alphas), jnp.stack(betas), out

    return jax.shard_map(
        local_fn,
        mesh=grid,
        in_specs=(psi_spec, P("core", None, None), P(("z", "yb", "ya", "x"), None, None), P()),
        out_specs=(P(), P(), psi_spec),
        check_vma=False,
    )
```

time: 2680 us -> 1630 us (0.61)
  waiting for transfers between devices: 1170 us -> 288 us
  blocking collectives: 1060 us -> 742 us
  between operations: 18.4 us -> 115 us
  matrix products: 225 us -> 307 us
    reduce_scatter x5 -> x0, waiting for transfers between devices: 1170 us -> none  [apply_ham(): lax.psum_scatter(part_out, 'right', scatter_dimension=3, tiled=True)]
    psum x16 -> x11, blocking collectives: 1040 us -> 729 us  [dots(): return lax.psum(jnp.stack(loc), ALL_AXES)]
    all_gather x0 -> x6, waiting for transfers between devices: none -> 279 us  [the longest x5 199 us: apply_ham(): full = lax.all_gather(vec, ROW_AXES, axis=0, tiled=True)]
    dot_general x15, matrix products: 225 us -> 307 us  [the longest x5 198 us: apply_ham(): jnp.einsum('cla,asb->lcsb', left_blk, full, precision=PREC_MODE, preferre...]
    dot_general x5 -> x0, local copies, waits for them, and re-layouts: 33.5 us -> none  [apply_ham(): jnp.einsum('rtvcb,bre->tvce', stage_two, env_right, precision=PREC_MODE,...]
    all_to_all x1 -> x6, local copies, waits for them, and re-layouts: 37 us -> 4.01 us  [the longest x3 3.04 us: local_fn(): psi = lax.all_to_all(psi_loc, ('ya', 'x'), 0, 3, tiled=True)]
    unnamed x8 -> x53, local copies, waits for them, and re-layouts: 37.2 us -> 64.1 us
  transfers between devices with their start and end apart: 6 -> 12, of which waited for: 5 -> 8; matrix products, arithmetic and copies ran while one was open for 0% -> 5% of each run, Pallas kernels for 0% -> 0%
where the time goes in v1:
time: 1630 us; the launch traced here: 1620 us
  blocking collectives  742 us (46%)
  matrix products  307 us (19%)
  waiting for transfers between devices  288 us (18%)
  between operations  115 us (7%)
  local copies, waits for them, and re-layouts  112 us (7%)
  other arithmetic  50.2 us (3%)
    psum x11, blocking collectives, dots(): return lax.psum(jnp.stack(loc), ALL_AXES)  729 us
    all_gather x5, waiting for transfers between devices, apply_ham(): full = lax.all_gather(vec, ROW_AXES, axis=0, tiled=True)  199 us
    dot_general x5, matrix products, apply_ham(): jnp.einsum('cla,asb->lcsb', left_blk, full, precision=PREC_MODE, preferre...  198 us
    dot_general x5, matrix products, apply_ham(): jnp.einsum('ctrb,bre->cte', t2, right_blk, precision=PREC_MODE, preferred...  84.4 us
    all_gather x1, waiting for transfers between devices, local_fn(): right_blk = lax.all_gather(env_right, ('ya', 'x'), axis=0, tiled=True)  80.2 us
    unnamed x53, local copies, waits for them, and re-layouts  64.1 us
    reduce_sum x12, other arithmetic, dots(): loc = [jnp.sum(b * vec) for b in basis] + [jnp.sum(p * q) for p, q in extra]  36 us
  transfers between devices with their start and end apart: 12, of which 8 were waited for; matrix products, arithmetic and copies ran while one was open for 5% of the time, Pallas kernels for 0%

profile of v1, /device:TPU:1, one launch (start us, length us, event | category | flops | bytes accessed | tf_op | source)
XLA Modules:
  0.0 1618.0 jit_solution(14023895845588883624)
XLA Ops:
  12.4 12.3 all_to_all.33
  35.0 4.8 constant_dynamic-slice_fusion
  39.7 36.5 %all-gather.7.cloned.1.call-done = f32[1536,4,192]{2,0,1:T(8,128)} async-done(((f32[96,4,192]{2,0,1:T(8,128)}), f32[1536,4,192]{2,0,1:T(8,128)}) %all-gather.7.cloned.1.call-update) | async-done | bytes 4718608 | tf_op jit(solution)/shard_map/all_gather | solution.py:32
  76.2 18.5 %fusion.18 = f32[96,8,4,192]{3,1,2,0:T(8,128)S(1)} fusion(f32[1536,4,192]{2,0,1:T(8,128)} %all-gather.7.cloned.1.call-done, f32[96,8,1536]{2,1,0:T(8,128)} %constant_dynamic-slice_fusion), kind=kOutput, calls=%fused_computation.18 | convolution fusion | flops 10871635968 | bytes 11796480 | tf_op jit(solution)/shard_map/cla,asb->lcsb/dot_general | solution.py:33
  99.2 80.2 %all-gather.9.cloned.1.call-done = f32[192,8,1536]{2,0,1:T(8,128)} async-done(((f32[24,8,1536]{2,0,1:T(8,128)}), f32[192,8,1536]{2,0,1:T(8,128)}) %all-gather.9.cloned.1.call-update) | async-done | bytes 9437200 | tf_op jit(solution)/shard_map/all_gather | solution.py:25
  179.4 24.5 %fusion.44 = f32[96,4,1536]{2,0,1:T(8,128)} fusion(f32[192,8,1536]{2,0,1:T(8,128)} %all-gather.9.cloned.1.call-done, f32[96,4,8,192]{3,2,1,0:T(8,128)} %fusion.81), kind=kOutput, calls=%fused_computation.44 | convolution fusion | flops 10871635968 | bytes 14155776 | tf_op jit(solution)/shard_map/ctrb,bre->cte/dot_general | solution.py:35
  204.0 4.5 copy.150
  208.4 4.5 reshape.51
  214.8 67.9 %psum.77 = f32[1]{0:T(128)} all-reduce(f32[1]{0:T(128)} %bitcast.4), channel_id=1, replica_groups=mesh['z'=4,'yb'=2,'ya'=2,'x'=4,'core'=2] {'z','yb','ya','x','core'}, use_global_device_ids=true, to_apply=%region_1.0 | all-reduce | flops 1 | bytes 8 | tf_op jit(solution)/shard_map/psum | solution.py:40
  283.4 4.6 reduce-scatter.16.cloned.1.call-done
  290.9 43.0 %all-gather.11.cloned.1.call-done = f32[1536,4,192]{2,1,0:T(4,128)} async-done(((f32[96,4,192]{2,1,0:T(4,128)}), f32[1536,4,192]{2,1,0:T(4,128)}) %all-gather.11.cloned.1.call-update) | async-done | bytes 4718608 | tf_op jit(solution)/shard_map/all_gather | solution.py:32
  333.9 44.9 %fusion.84 = f32[8,96,4,192,1]{1,3,0,2,4:T(8,128)S(1)} fusion(f32[96,8,1536]{2,1,0:T(8,128)} %constant_dynamic-slice_fusion, f32[1536,4,192,1]{2,1,0,3:T(4,128)} %bitcast.313), kind=kOutput, calls=%fused_computation.54 | convolution fusion | flops 10871635968 | bytes 11796480 | tf_op jit(solution)/shard_map/cla,asb->lcsb/dot_general | solution.py:33
  378.7 4.9 fusion.69
  383.7 14.9 fusion.49
  398.6 4.5 copy.152
  403.1 4.5 reshape.53
  409.7 68.5 %psum.78 = f32[2]{0:T(128)S(1)} all-reduce(f32[2]{0:T(128)S(1)} %pad_maximum_fusion), channel_id=1, replica_groups=mesh['z'=4,'yb'=2,'ya'=2,'x'=4,'core'=2] {'z','yb','ya','x','core'}, use_global_device_ids=true, to_apply=%region_5.0 | all-reduce | flops 2 | bytes 16 | tf_op jit(solution)/shard_map/psum | solution.py:40
  481.5 64.5 %psum.79 = f32[2]{0:T(128)S(1)} all-reduce(f32[2]{0:T(128)S(1)} %pad_maximum_fusion.1), channel_id=1, replica_groups=mesh['z'=4,'yb'=2,'ya'=2,'x'=4,'core'=2] {'z','yb','ya','x','core'}, use_global_device_ids=true, to_apply=%region_9.0 | all-reduce | flops 2 | bytes 16 | tf_op jit(solution)/shard_map/psum | solution.py:40
  556.7 39.2 %all-gather.13.cloned.1.call-done = f32[1536,4,192]{2,1,0:T(4,128)} async-done(((f32[96,4,192]{2,1,0:T(4,128)}), f32[1536,4,192]{2,1,0:T(4,128)}) %all-gather.13.cloned.1.call-update) | async-done | bytes 4718608 | tf_op jit(solution)/shard_map/all_gather | solution.py:32
  595.9 44.9 %fusion.89 = f32[8,96,4,192,1]{1,3,0,2,4:T(8,128)S(1)} fusion(f32[96,8,1536]{2,1,0:T(8,128)} %constant_dynamic-slice_fusion, f32[1536,4,192,1]{2,1,0,3:T(4,128)} %bitcast.314), kind=kOutput, calls=%fused_computation.55 | convolution fusion | flops 10871635968 | bytes 11796480 | tf_op jit(solution)/shard_map/cla,asb->lcsb/dot_general | solution.py:33
  640.8 4.9 fusion.72
  645.8 15.1 fusion.54
  660.9 4.5 copy.154
  672.5 70.6 %psum.80 = f32[4]{0:T(128)S(1)} all-reduce(f32[4]{0:T(128)S(1)} %pad_maximum_fusion.2), channel_id=1, replica_groups=mesh['z'=4,'yb'=2,'ya'=2,'x'=4,'core'=2] {'z','yb','ya','x','core'}, use_global_device_ids=true, to_apply=%region_14.0 | all-reduce | flops 4 | bytes 32 | tf_op jit(solution)/shard_map/psum | solution.py:40
  748.5 64.4 %psum.81 = f32[3]{0:T(128)S(1)} all-reduce(f32[3]{0:T(128)S(1)} %pad_maximum_fusion.3), channel_id=1, replica_groups=mesh['z'=4,'yb'=2,'ya'=2,'x'=4,'core'=2] {'z','yb','ya','x','core'}, use_global_device_ids=true, to_apply=%region_19.0 | all-reduce | flops 3 | bytes 24 | tf_op jit(solution)/shard_map/psum | solution.py:40
  831.3 40.1 %all-gather.15.cloned.1.call-done = f32[1536,4,192]{2,1,0:T(4,128)} async-done(((f32[96,4,192]{2,1,0:T(4,128)}), f32[1536,4,192]{2,1,0:T(4,128)}) %all-gather.15.cloned.1.call-update) | async-done | bytes 4718608 | tf_op jit(solution)/shard_map/all_gather | solution.py:32
  871.4 44.9 %fusion.94 = f32[8,96,4,192,1]{1,3,0,2,4:T(8,128)S(1)} fusion(f32[96,8,1536]{2,1,0:T(8,128)} %constant_dynamic-slice_fusion, f32[1536,4,192,1]{2,1,0,3:T(4,128)} %bitcast.315), kind=kOutput, calls=%fused_computation.56 | convolution fusion | flops 10871635968 | bytes 11796480 | tf_op jit(solution)/shard_map/cla,asb->lcsb/dot_general | solution.py:33
  916.3 4.9 fusion.75
  921.2 14.9 fusion.59
  936.1 4.5 copy.156
  949.0 69.8 %psum.82 = f32[6]{0:T(128)S(1)} all-reduce(f32[6]{0:T(128)S(1)} %stack.226), channel_id=1, replica_groups=mesh['z'=4,'yb'=2,'ya'=2,'x'=4,'core'=2] {'z','yb','ya','x','core'}, use_global_device_ids=true, to_apply=%region_26.0 | all-reduce | flops 6 | bytes 48 | tf_op jit(solution)/shard_map/psum | solution.py:40
  1025.6 63.7 %psum.83 = f32[4]{0:T(128)S(1)} all-reduce(f32[4]{0:T(128)S(1)} %pad_maximum_fusion.4), channel_id=1, replica_groups=mesh['z'=4,'yb'=2,'ya'=2,'x'=4,'core'=2] {'z','yb','ya','x','core'}, use_global_device_ids=true, to_apply=%region_32.0 | all-reduce | flops 4 | bytes 32 | tf_op jit(solution)/shard_map/psum | solution.py:40
  1111.4 5.1 multiply_reduce_fusion.21
  1118.6 40.0 %all-gather.17.cloned.1.call-done = f32[1536,4,192]{2,1,0:T(4,128)} async-done(((f32[96,4,192]{2,1,0:T(4,128)}), f32[1536,4,192]{2,1,0:T(4,128)}) %all-gather.17.cloned.1.call-update) | async-done | bytes 4718608 | tf_op jit(solution)/shard_map/all_gather | solution.py:32
  1158.6 44.9 %fusion.99 = f32[8,96,4,192,1]{1,3,0,2,4:T(8,128)S(1)} fusion(f32[96,8,1536]{2,1,0:T(8,128)} %constant_dynamic-slice_fusion, f32[1536,4,192,1]{2,1,0,3:T(4,128)} %bitcast.312), kind=kOutput, calls=%fused_computation.57 | convolution fusion | flops 10871635968 | bytes 11796480 | tf_op jit(solution)/shard_map/cla,asb->lcsb/dot_general | solution.py:33
  1203.5 4.9 fusion.78
  1208.5 14.9 fusion.64
  1223.4 4.5 copy.158
  1227.9 4.5 reshape.59
  1232.5 5.0 stack.240
  1237.5 70.0 %psum.84 = f32[8]{0:T(128)S(1)} all-reduce(f32[8]{0:T(128)S(1)} %stack.240), channel_id=1, replica_groups=mesh['z'=4,'yb'=2,'ya'=2,'x'=4,'core'=2] {'z','yb','ya','x','core'}, use_global_device_ids=true, to_apply=%region_41.0 | all-reduce | flops 8 | bytes 64 | tf_op jit(solution)/shard_map/psum | solution.py:40
  1315.6 63.2 %psum.85 = f32[5]{0:T(128)S(1)} all-reduce(f32[5]{0:T(128)S(1)} %stack.246), channel_id=1, replica_groups=mesh['z'=4,'yb'=2,'ya'=2,'x'=4,'core'=2] {'z','yb','ya','x','core'}, use_global_device_ids=true, to_apply=%region_48.0 | all-reduce | flops 5 | bytes 40 | tf_op jit(solution)/shard_map/psum | solution.py:40
  1410.3 5.8 multiply_reduce_fusion.6
  1416.1 6.2 stack.257
  1422.3 64.3 %psum.86 = f32[10]{0:T(128)S(1)} all-reduce(f32[10]{0:T(128)S(1)} %stack.257), channel_id=1, replica_groups=mesh['z'=4,'yb'=2,'ya'=2,'x'=4,'core'=2] {'z','yb','ya','x','core'}, use_global_device_ids=true, to_apply=%region_59.0 | all-reduce | flops 10 | bytes 80 | tf_op jit(solution)/shard_map/psum | solution.py:40
  1487.3 5.1 multiply_reduce_fusion
  1496.2 62.5 %psum.87 = f32[6]{0:T(128)S(1)} all-reduce(f32[6]{0:T(128)S(1)} %stack.269), channel_id=1, replica_groups=mesh['z'=4,'yb'=2,'ya'=2,'x'=4,'core'=2] {'z','yb','ya','x','core'}, use_global_device_ids=true, to_apply=%region_66.0 | all-reduce | flops 6 | bytes 48 | tf_op jit(solution)/shard_map/psum | solution.py:40
  1605.7 4.5 all-to-all-done.1
  (121 shorter events, 103.5 us)
Async XLA Ops:
  7.2 69.1 %all-gather.7.cloned.1.call-start = ((), (), s32[]{:S(2)}) async-start(), calls=%async_computation.7 | async-start | bytes 6684672 | tf_op jit(solution)/shard_map/all_gather | solution.py:32
  29.1 5.7 copy-start.4
  31.6 147.9 %all-gather.9.cloned.1.call-start = ((), (), s32[]{:S(2)}) async-start(), calls=%async_computation.8 | async-start | bytes 10616832 | tf_op jit(solution)/shard_map/all_gather | solution.py:25
  34.6 253.3 %reduce-scatter.16.cloned.1.call-start = ((), (), s32[]{:S(2)}) async-start(), calls=%async_computation.13 | async-start | bytes 2654208
  212.9 120.9 %all-gather.11.cloned.1.call-start = ((), (), s32[]{:S(2)}) async-start(), calls=%async_computation.9 | async-start | bytes 6684672 | tf_op jit(solution)/shard_map/all_gather | solution.py:32
  289.9 93.8 %slice-start = ((s8[9437184]{0:T(1024)(128)(4,1)}), s8[1048576]{0:T(1024)(128)(4,1)S(1)}, s32[]{:S(2)}) async-start(s8[9437184]{0:T(1024)(128)(4,1)} %bitcast.277), calls=%async_computation.18 | async-start | bytes 2097152
  290.8 261.3 %reduce-scatter.18.cloned.1.call-start = ((), (), s32[]{:S(2)}) async-start(), calls=%async_computation.14 | async-start | bytes 2654208
  333.9 49.8 %slice-start.1 = ((s8[9437184]{0:T(1024)(128)(4,1)}), s8[4194304]{0:T(1024)(128)(4,1)S(1)}, s32[]{:S(2)}) async-start(s8[9437184]{0:T(1024)(128)(4,1)} %bitcast.277), calls=%async_computation.19 | async-start | bytes 8388608
  333.9 49.8 %slice-start.2 = ((s8[9437184]{0:T(1024)(128)(4,1)}), s8[4194304]{0:T(1024)(128)(4,1)S(1)}, s32[]{:S(2)}) async-start(s8[9437184]{0:T(1024)(128)(4,1)} %bitcast.277), calls=%async_computation.20 | async-start | bytes 8388608
  407.6 188.3 %all-gather.13.cloned.1.call-start = ((), (), s32[]{:S(2)}) async-start(), calls=%async_computation.10 | async-start | bytes 6684672 | tf_op jit(solution)/shard_map/all_gather | solution.py:32
  555.7 90.1 %slice-start.3 = ((s8[9437184]{0:T(1024)(128)(4,1)}), s8[1048576]{0:T(1024)(128)(4,1)S(1)}, s32[]{:S(2)}) async-start(s8[9437184]{0:T(1024)(128)(4,1)} %bitcast.279), calls=%async_computation.21 | async-start | bytes 2097152
  556.6 268.2 %reduce-scatter.20.cloned.1.call-start = ((), (), s32[]{:S(2)}) async-start(), calls=%async_computation.15 | async-start | bytes 2654208
  595.9 49.9 %slice-start.4 = ((s8[9437184]{0:T(1024)(128)(4,1)}), s8[4194304]{0:T(1024)(128)(4,1)S(1)}, s32[]{:S(2)}) async-start(s8[9437184]{0:T(1024)(128)(4,1)} %bitcast.279), calls=%async_computation.22 | async-start | bytes 8388608
  595.9 49.9 %slice-start.5 = ((s8[9437184]{0:T(1024)(128)(4,1)}), s8[4194304]{0:T(1024)(128)(4,1)S(1)}, s32[]{:S(2)}) async-start(s8[9437184]{0:T(1024)(128)(4,1)} %bitcast.279), calls=%async_computation.23 | async-start | bytes 8388608
  669.9 201.5 %all-gather.15.cloned.1.call-start = ((), (), s32[]{:S(2)}) async-start(), calls=%async_computation.11 | async-start | bytes 6684672 | tf_op jit(solution)/shard_map/all_gather | solution.py:32
  826.8 94.4 %slice-start.6 = ((s8[9437184]{0:T(1024)(128)(4,1)}), s8[1048576]{0:T(1024)(128)(4,1)S(1)}, s32[]{:S(2)}) async-start(s8[9437184]{0:T(1024)(128)(4,1)} %bitcast.281), calls=%async_computation.24 | async-start | bytes 2097152
  830.2 189.3 %copy-start = (f32[96,4,192]{0,2,1:T(8,128)}, f32[96,4,192]{0,2,1:T(8,128)S(1)}, u32[]{:S(2)}) copy-start(f32[96,4,192]{0,2,1:T(8,128)S(1)} %get-tuple-element.58) | copy-start | bytes 884740
  831.2 278.2 %reduce-scatter.22.cloned.1.call-start = ((), (), s32[]{:S(2)}) async-start(), calls=%async_computation.16 | async-start | bytes 2654208
  871.4 49.8 %slice-start.7 = ((s8[9437184]{0:T(1024)(128)(4,1)}), s8[4194304]{0:T(1024)(128)(4,1)S(1)}, s32[]{:S(2)}) async-start(s8[9437184]{0:T(1024)(128)(4,1)} %bitcast.281), calls=%async_computation.25 | async-start | bytes 8388608
  871.4 49.8 %slice-start.8 = ((s8[9437184]{0:T(1024)(128)(4,1)}), s8[4194304]{0:T(1024)(128)(4,1)S(1)}, s32[]{:S(2)}) async-start(s8[9437184]{0:T(1024)(128)(4,1)} %bitcast.281), calls=%async_computation.26 | async-start | bytes 8388608
  945.1 213.5 %all-gather.17.cloned.1.call-start = ((), (), s32[]{:S(2)}) async-start(), calls=%async_computation.12 | async-start | bytes 6684672 | tf_op jit(solution)/shard_map/all_gather | solution.py:32
  1111.4 97.0 %slice-start.9 = ((s8[9437184]{0:T(1024)(128)(4,1)}), s8[1048576]{0:T(1024)(128)(4,1)S(1)}, s32[]{:S(2)}) async-start(s8[9437184]{0:T(1024)(128)(4,1)} %bitcast.283), calls=%async_computation.27 | async-start | bytes 2097152
  1118.5 289.8 %reduce-scatter.24.cloned.1.call-start = ((), (), s32[]{:S(2)}) async-start(), calls=%async_computation.17 | async-start | bytes 2654208
  1158.6 49.9 %slice-start.10 = ((s8[9437184]{0:T(1024)(128)(4,1)}), s8[4194304]{0:T(1024)(128)(4,1)S(1)}, s32[]{:S(2)}) async-start(s8[9437184]{0:T(1024)(128)(4,1)} %bitcast.283), calls=%async_computation.28 | async-start | bytes 8388608
  1158.6 49.9 %slice-start.11 = ((s8[9437184]{0:T(1024)(128)(4,1)}), s8[4194304]{0:T(1024)(128)(4,1)S(1)}, s32[]{:S(2)}) async-start(s8[9437184]{0:T(1024)(128)(4,1)} %bitcast.283), calls=%async_computation.29 | async-start | bytes 8388608
  1227.9 80.2 %copy-start.2 = (f32[96,4,192]{0,2,1:T(8,128)S(1)}, f32[96,4,192]{0,2,1:T(8,128)}, u32[]{:S(2)}) copy-start(f32[96,4,192]{0,2,1:T(8,128)} %get-tuple-element.55) | copy-start | bytes 884740
  1232.5 177.9 %copy-start.1 = (f32[96,4,192]{0,2,1:T(8,128)S(1)}, f32[96,4,192]{0,2,1:T(8,128)}, u32[]{:S(2)}) copy-start(f32[96,4,192]{0,2,1:T(8,128)} %copy-done) | copy-start | bytes 884740
  1416.1 177.6 %copy-start.3 = (f32[96,4,192]{0,2,1:T(8,128)S(1)}, f32[96,4,192]{0,2,1:T(8,128)}, u32[]{:S(2)}) copy-start(f32[96,4,192]{0,2,1:T(8,128)} %get-tuple-element.53) | copy-start | bytes 884740
  1598.0 12.3 all-to-all-start.1
Sparse Core Ops, SparseCore 0:
  31.7 44.5 all-gather.6
  77.9 101.4 all-gather.8
  213.1 74.8 reduce-scatter.15
  290.9 42.8 all-gather.10
  407.7 76.1 reduce-scatter.17
  556.7 39.1 all-gather.12
  670.0 75.9 reduce-scatter.19
  831.3 40.0 all-gather.14
  945.2 75.7 reduce-scatter.21
  1118.7 39.8 all-gather.16
  1232.6 76.3 reduce-scatter.23

commit v2 on v0

v2 whole, which is shorter than its diff:
```python
import functools
import math

import jax
import jax.numpy as jnp
from jax import lax
from jax.experimental import pallas as pl
from jax.experimental.pallas import tpu as pltpu
from jax.sharding import Mesh
from jax.sharding import PartitionSpec as P

STEPS = 5
AXES = ("z", "yb", "ya", "x", "core")
F32, BF16 = jnp.float32, jnp.bfloat16
MESH = pl.DeviceIdType.MESH
D = 1536
HALF = 48
NCH = 6
LANE = 128
WIDE = 256
MROWS = 768


def split3(val):
    hi = val.astype(BF16)
    rest = val - hi.astype(F32)
    mid = rest.astype(BF16)
    low = (rest - mid.astype(F32)).astype(BF16)
    return hi, mid, low


def swap(val):
    return pltpu.roll(val, 64, axis=val.ndim - 1)


def low_half(shape):
    return lax.broadcasted_iota(jnp.int32, shape, len(shape) - 1) < 64


def dot(a, b):
    return jnp.dot(a, b, preferred_element_type=F32)


def dot6(a, b, k):
    return dot(a[...], b[...]) + dot(a[:, : 2 * k], b[k:, :]) + dot(a[:, :k], b[2 * k :, :])


def mult(val, n):
    return pl.multiple_of(val, n)


def seg(i, size):
    return slice(i * size, (i + 1) * size)


def row1(i):
    return slice(i, i + 1)


def wide(val):
    return jnp.concatenate([val, val], axis=1)


def pair_halves(e, o):
    lo = low_half(e.shape)
    return jnp.where(lo, e, swap(o)), jnp.where(lo, swap(e), o)


def fold(val):
    return jnp.sum(val.reshape(-1, 8, LANE), axis=0)


def kernel(
    psi_ref, mix_ref, el_ref, rg_ref, v_out, a_out, b_out,
    l3, r3, w3, gb, v3, t1, tq, t2, o3, sb, rsb, xs, vs, u1, stage, dots, ra, rb, cg, gam, gram,
    rs_recv, rs_send, ag_recv, ag_send, fw_recv, fw_send, ra_recv, ra_send, rb_recv, rb_send, st_sem,
):
    z, yb, ya, x, core = (lax.axis_index(name) for name in AXES)
    row = lax.rem(ya + yb, 2)
    ia8 = row * 4 + x
    ia = core * 8 + ia8
    ib = z * 2 + yb

    def a_peer(d, other):
        to_row = lax.rem(row + d // 4, 2)
        return {"z": z, "yb": yb, "ya": lax.rem(to_row + yb, 2), "x": lax.rem(x + d % 4, 4), "core": 1 - core if other else core}

    def b_peer(d):
        to_yb = lax.rem(yb + d // 4, 2)
        return {"z": lax.rem(z + d % 4, 4), "yb": to_yb, "ya": lax.rem(row + to_yb, 2), "x": x, "core": core}

    def b_index(d):
        return lax.rem(z + d % 4, 4) * 2 + lax.rem(yb + d // 4, 2)

    partner = a_peer(0, True)
    a_peers = [a_peer(d, False) for d in range(1, 8)] + [a_peer(d, True) for d in range(8)]
    b_peers = [b_peer(d) for d in range(1, 8)]

    barrier = pltpu.get_barrier_semaphore()
    for peer in a_peers + b_peers:
        pl.semaphore_signal(barrier, inc=1, device_id=peer, device_id_type=MESH)
    pl.semaphore_wait(barrier, len(a_peers) + len(b_peers))

    def remote(src, dst, send, recv, peer):
        return pltpu.make_async_remote_copy(src_ref=src, dst_ref=dst, send_sem=send, recv_sem=recv, device_id=peer, device_id_type=MESH)

    def wait_bytes(ref, sem):
        pltpu.make_async_copy(ref, ref, sem).wait()

    def ag_start(par, k):
        mine = gb.at[par, k, ia]
        for d in range(1, 8):
            remote(mine, mine, ag_send.at[k], ag_recv.at[par, k], a_peer(d, False)).start()

    def ag_forward(par, k, m):
        wait_bytes(rsb.at[0, k], ag_recv.at[par, k])

        @pl.when(m > 0)
        def _():
            wait_bytes(gb.at[0, k, pl.ds(0, 8)], fw_send.at[k])

        part = gb.at[par, k, pl.ds(core * 8, 8)]
        remote(part, part, fw_send.at[k], fw_recv.at[par, k], partner).start()

    def rs_start(par, k):
        for d in range(1, 8):
            remote(sb.at[k, b_index(d)], rsb.at[par, k, d - 1], rs_send.at[k], rs_recv.at[par, k], b_peers[d - 1]).start()

    def publish(m, k, first):
        par = lax.rem(m, 2)
        if not first:
            wait_bytes(rsb.at[0, k], ag_send.at[k])
        gb[par, k, ia] = xs[m, k]
        ag_start(par, k)

    def combine(m, k):
        prev = lax.rem(m + 1, 2)
        wait_bytes(rsb.at[prev, k], rs_recv.at[prev, k])
        w = sb[k, ib]
        for d in range(7):
            w = w + rsb[prev, k, d]
        for i in range(STEPS):
            w = w - wide(gam[row1(i), :]) * xs[i + 1, k]
        xs[m, k] = w * wide(gam[row1(STEPS), :])

    def local_dots(m, k):
        last = jnp.maximum(m - 1, 0)
        cur = xs[m, k]
        new = vs[last, k]
        for i in range(STEPS):
            vec = vs[i, k]
            dots[i] = dots[i] + fold(vec * cur)
            dots[5 + i] = dots[5 + i] + fold(vec * new)

    def red_rows(which, pairs):
        ra[which, ia] = jnp.zeros((16, LANE), F32)
        for src, dst in pairs:
            ra[which, ia, row1(dst), :] = jnp.sum(dots[src], axis=0, keepdims=True)
        mine = ra.at[which, ia]
        for peer in a_peers:
            remote(mine, mine, ra_send.at[which], ra_recv.at[which], peer).start()

    def red_mid(which):
        wait_bytes(ra.at[which, pl.ds(0, 15)], ra_recv.at[which])
        wait_bytes(ra.at[which, pl.ds(0, 15)], ra_send.at[which])
        total = ra[which, 0]
        for i in range(1, 16):
            total = total + ra[which, i]
        rb[which, ib] = total
        mine = rb.at[which, ib]
        for peer in b_peers:
            remote(mine, mine, rb_send.at[which], rb_recv.at[which], peer).start()

    def red_end(which):
        wait_bytes(rb.at[which, pl.ds(0, 7)], rb_recv.at[which])
        wait_bytes(rb.at[which, pl.ds(0, 7)], rb_send.at[which])
        total = rb[which, 0]
        for i in range(1, 8):
            total = total + rb[which, i]
        return jnp.broadcast_to(jnp.sum(total, axis=1, keepdims=True), (16, LANE))

    def red1_start():
        red_rows(0, [(i, i) for i in range(5)] + [(5 + i, 8 + i) for i in range(5)])
        dots[...] = jnp.zeros_like(dots)

    def red1_end(m):
        total = red_end(0)
        cg[...] = total[0:8]
        gram[jnp.maximum(m - 1, 0)] = total[8:16]
        a_out[m] = total[0:8]

        def piece(k, _):
            cur = xs[m, k]
            for i in range(STEPS):
                cur = cur - wide(cg[row1(i), :]) * vs[i, k]
            u1[k] = cur
            for i in range(STEPS):
                dots[i] = dots[i] + fold(vs[i, k] * cur)
            dots[5] = dots[5] + fold(cur * cur)
            return 0

        lax.fori_loop(0, NCH, piece, 0)
        red_rows(1, [(i, i) for i in range(5)] + [(5, 8)])
        dots[...] = jnp.zeros_like(dots)

    def red2_end(m, last):
        total = red_end(1)
        d8 = total[0:8]
        sq = total[8:9]
        for i in range(STEPS):
            di = d8[row1(i)]
            inner = jnp.sum(d8 * gram[i], axis=0, keepdims=True)
            sq = sq - 2.0 * di * di + di * (2.0 * inner - di * gram[i, row1(i), :])
        beta = jnp.sqrt(sq)
        inv = 1.0 / beta
        b_out[m] = jnp.broadcast_to(beta, (8, LANE))
        gam[...] = cg[...] + d8
        gam[row1(STEPS), :] = inv
        scale = inv * math.sqrt(float(4 * D * D)) if last else inv
        scale = wide(scale)

        def piece(k, _):
            cur = u1[k]
            for i in range(STEPS):
                cur = cur - wide(d8[row1(i)]) * vs[i, k]
            if last:
                v_out[k] = cur * scale
            else:
                vs[m, k] = cur * scale
            return 0

        lax.fori_loop(0, NCH, piece, 0)

    def split_chunk(par, n):
        def piece(i, _):
            for h in range(2):
                r = mult(i * 96 + h * HALF, 16)
                for part, val in enumerate(reversed(split3(gb[par, 2 * n + h, i]))):
                    v3[pl.ds(part * D + r, HALF), :] = val
            return 0

        lax.fori_loop(0, 16, piece, 0)

    def mix_chunk(n):
        def quad(q, _):
            r0 = mult(q * 256, 256)
            xg = [t1[pl.ds(r0 + 64 * i, 64), :] for i in range(4)]
            for p in range(2):
                for sp in range(2):
                    e, o = (xg[2 * p + i][:, seg(sp, LANE)] for i in range(2))
                    for s, val in enumerate(pair_halves(e, o)):
                        for part, piece in enumerate(reversed(split3(val))):
                            tq[seg(4 * part + 2 * sp + s, 64), seg(p, LANE)] = piece
            out = dot6(w3, tq, WIDE)
            for p in range(2):
                pp = 2 * q + p
                h = pp // 3
                base = h * 192 + (pp - 3 * h) * 16
                for t in range(4):
                    r = mult(base + t * HALF, 16)
                    for rp in range(4):
                        e, f = (out[seg(8 * t + 2 * rp + i, 8), seg(p, LANE)] for i in range(2))
                        g = jnp.concatenate(pair_halves(e, f), axis=0)
                        for part, val in enumerate(split3(g)):
                            t2[pl.ds(r, 16), pl.ds(mult(part * D + n * 512 + rp * LANE, LANE), LANE)] = val
            return 0

        lax.fori_loop(0, 3, quad, 0)

    def out_chunk(m, k):
        n = k // 2
        h = k - 2 * n
        o3[...] = dot6(t2.at[pl.ds(mult(h * 192, 192), 192)], r3.at[:, pl.ds(mult(n * 512, 512), 512)], D)

        @pl.when(m > 0)
        def _():
            wait_bytes(rsb.at[0, k], rs_send.at[k])

        for j in range(4):
            y = [o3[seg(t, HALF), seg(j, LANE)] for t in range(4)]
            for sp in range(2):
                for i, val in enumerate(pair_halves(y[2 * sp], y[2 * sp + 1])):
                    sb[k, 2 * j + i, :, seg(sp, LANE)] = val
        rs_start(lax.rem(m, 2), k)

    def init(k, _):
        for i in range(STEPS):
            xs[i + 1, k] = jnp.zeros((HALF, WIDE), F32)
            vs[i, k] = jnp.zeros((HALF, WIDE), F32)
        xs[0, k] = psi_ref[k]
        return 0

    lax.fori_loop(0, NCH, init, 0)
    dots[...] = jnp.zeros_like(dots)
    gram[...] = jnp.zeros_like(gram)
    gam[...] = jnp.zeros_like(gam)
    for k in range(4):
        publish(0, k, True)
        local_dots(0, k)
    for part, val in enumerate(split3(mix_ref[...])):
        w3[:, seg(part, WIDE)] = val

    def el_copy(i, slot):
        return pltpu.make_async_copy(el_ref.at[pl.ds(mult(ia8 * 768 + i * HALF, HALF), HALF)], stage.at[slot], st_sem.at[slot, 0])

    el_copy(0, 0).start()

    def el_piece(i, _):
        slot = lax.rem(i, 2)

        @pl.when(i < 15)
        def _():
            el_copy(i + 1, 1 - slot).start()

        el_copy(i, slot).wait()
        for c in range(6):
            for part, val in enumerate(split3(stage[slot, :, seg(c, WIDE)])):
                l3[pl.ds(mult(i * HALF, 16), HALF), seg(6 * part + c, WIDE)] = val
        return 0

    lax.fori_loop(0, 16, el_piece, 0)

    def rg_copy(i, slot, half):
        mp = i // 8
        r = i - 8 * mp
        return pltpu.make_async_copy(
            rg_ref.at[pl.ds(mult(((2 * mp + half) * 8 + r) * 24, 24), 24)],
            stage.at[slot, pl.ds(half * 24, 24)],
            st_sem.at[slot, half],
        )

    for half in range(2):
        rg_copy(0, 0, half).start()

    def rg_piece(i, _):
        slot = lax.rem(i, 2)

        @pl.when(i < 31)
        def _():
            for half in range(2):
                rg_copy(i + 1, 1 - slot, half).start()

        for half in range(2):
            rg_copy(i, slot, half).wait()
        mp = i // 8
        r = i - 8 * mp
        lo = low_half((16, LANE))
        for g in range(3):
            bg = 3 * mp + g
            n = bg // 4
            dst = mult(n * 512 + r * 64 + (bg - 4 * n) * 16, 16)
            for j in range(4):
                tl = [stage[slot, seg(g, 16), seg(3 * j + c, LANE)] for c in range(3)]
                new = (jnp.where(lo, tl[0], tl[1]), swap(jnp.where(lo, tl[2], tl[0])), jnp.where(lo, tl[1], tl[2]))
                for c in range(3):
                    for part, val in enumerate(reversed(split3(new[c]))):
                        r3[pl.ds(part * D + dst, 16), seg(4 * c + j, LANE)] = val
        return 0

    lax.fori_loop(0, 32, rg_piece, 0)

    def step(m, _):
        par = lax.rem(m, 2)

        def chunk(n, _):
            ag_forward(par, 2 * n, m)
            ag_forward(par, 2 * n + 1, m)

            @pl.when(n < 2)
            def _():
                k = 4 + n

                @pl.when(m > 0)
                def _():
                    combine(m, k)
                    wait_bytes(rsb.at[0, k], ag_send.at[k])

                gb[par, k, ia] = xs[m, k]
                ag_start(par, k)
                local_dots(m, k)

            @pl.when(n == 1)
            def _():
                red1_start()

            for h in range(2):
                wait_bytes(gb.at[par, 2 * n + h, pl.ds((1 - core) * 8, 8)], fw_recv.at[par, 2 * n + h])
            split_chunk(par, n)
            t1[...] = dot6(l3, v3, D)
            mix_chunk(n)

            @pl.when(n == 1)
            def _():
                red_mid(0)

            return 0

        lax.fori_loop(0, 3, chunk, 0)
        red1_end(m)

        def outs(k, _):
            out_chunk(m, k)

            @pl.when(k == 2)
            def _():
                red_mid(1)

            return 0

        lax.fori_loop(0, NCH, outs, 0)
        red2_end(m, False)

        def head(k, _):
            combine(m + 1, k)
            local_dots(m + 1, k)

            @pl.when(m < STEPS - 1)
            def _():
                publish(m + 1, k, False)

            return 0

        lax.fori_loop(0, 4, head, 0)
        return 0

    lax.fori_loop(0, STEPS, step, 0)

    def tail(k, _):
        combine(STEPS, k)
        local_dots(STEPS, k)
        return 0

    lax.fori_loop(4, NCH, tail, 0)
    red1_start()
    red_mid(0)
    red1_end(STEPS)
    red_mid(1)
    red2_end(STEPS, True)
    for k in range(NCH):
        wait_bytes(rsb.at[0, k], ag_send.at[k])
        wait_bytes(rsb.at[0, k], rs_send.at[k])
        wait_bytes(gb.at[0, k, pl.ds(0, 8)], fw_send.at[k])


def run_kernel(psi, mix, el, rg):
    vmem = pl.BlockSpec(memory_space=pltpu.VMEM)
    hbm = pl.BlockSpec(memory_space=pl.ANY)
    dma = pltpu.SemaphoreType.DMA
    return pl.pallas_call(
        kernel,
        out_shape=(
            jax.ShapeDtypeStruct((NCH, HALF, WIDE), F32),
            jax.ShapeDtypeStruct((STEPS + 1, 8, LANE), F32),
            jax.ShapeDtypeStruct((STEPS + 1, 8, LANE), F32),
        ),
        in_specs=[vmem, vmem, hbm, hbm],
        out_specs=(vmem, vmem, vmem),
        scratch_shapes=[
            pltpu.VMEM((MROWS, 3 * D), BF16),
            pltpu.VMEM((3 * D, D), BF16),
            pltpu.VMEM((WIDE, MROWS), BF16),
            pltpu.VMEM((2, NCH, 16, HALF, WIDE), F32),
            pltpu.VMEM((3 * D, WIDE), BF16),
            pltpu.VMEM((MROWS, WIDE), F32),
            pltpu.VMEM((MROWS, WIDE), BF16),
            pltpu.VMEM((384, 3 * D), BF16),
            pltpu.VMEM((192, 512), F32),
            pltpu.VMEM((NCH, 8, HALF, WIDE), F32),
            pltpu.VMEM((2, NCH, 7, HALF, WIDE), F32),
            pltpu.VMEM((STEPS + 1, NCH, HALF, WIDE), F32),
            pltpu.VMEM((STEPS, NCH, HALF, WIDE), F32),
            pltpu.VMEM((NCH, HALF, WIDE), F32),
            pltpu.VMEM((2, HALF, D), F32),
            pltpu.VMEM((10, 8, LANE), F32),
            pltpu.VMEM((2, 16, 16, LANE), F32),
            pltpu.VMEM((2, 8, 16, LANE), F32),
            pltpu.VMEM((8, LANE), F32),
            pltpu.VMEM((8, LANE), F32),
            pltpu.VMEM((STEPS, 8, LANE), F32),
            dma((2, NCH)), dma((NCH,)), dma((2, NCH)), dma((NCH,)), dma((2, NCH)), dma((NCH,)),
            dma((2,)), dma((2,)), dma((2,)), dma((2,)), dma((2, 2)),
        ],
        compiler_params=pltpu.CompilerParams(collective_id=0, has_side_effects=True, vmem_limit_bytes=67043328),
        name="lanczos",
    )(psi, mix, el, rg)


def solution(mesh):
    grid = Mesh(mesh.devices.reshape(4, 2, 2, 4, 2), AXES)
    psi_spec = P("core", None, None, ("z", "yb", "ya", "x"))

    def local_fn(psi_loc, env_left, env_right, mpo_pair):
        odd = lax.axis_index("yb") == 1

        def swap_rows(val):
            return jnp.where(odd, jnp.roll(val, 384, axis=0), val)

        rg = lax.all_gather(jnp.transpose(env_right, (1, 0, 2)), ("ya", "x"), axis=0, tiled=True).reshape(D, D)
        psi = lax.all_to_all(swap_rows(psi_loc.reshape(768, 4, 24)), ("ya", "x"), 0, 2, tiled=True)
        psi = psi.reshape(2, HALF, 4, 3, 64).transpose(3, 0, 1, 2, 4).reshape(NCH, HALF, WIDE)
        w = mpo_pair.reshape(8, 8, 4, 4)
        mix = jnp.einsum("lrst,ab->trasbl", w, jnp.eye(8, dtype=F32), precision=lax.Precision.HIGHEST).reshape(256, 256)
        vec, aa, bb = run_kernel(psi, mix, env_left.reshape(6144, D), rg)
        out = vec.reshape(3, 2, HALF, 4, 64).transpose(1, 2, 3, 0, 4).reshape(96, 4, 192)
        out = swap_rows(lax.all_to_all(out, ("ya", "x"), 2, 0, tiled=True)).reshape(768, 2, 2, 24)
        alpha = jnp.stack([aa[i + 1, i, 0] for i in range(STEPS)])
        return alpha, bb[1:, 0, 0], out

    return jax.shard_map(
        local_fn,
        mesh=grid,
        in_specs=(psi_spec, P("core", None, None), P(("z", "yb", "ya", "x"), None, None), P()),
        out_specs=(P(), P(), psi_spec),
        check_vma=False,
    )
```

time: 2680 us -> 506 us (0.19)
  waiting for transfers between devices: 1170 us -> 83.3 us
  blocking collectives: 1060 us -> 0 us
  Pallas kernels: 0 us -> 351 us
  matrix products: 225 us -> 0 us
  local copies, waits for them, and re-layouts: 123 us -> 40.9 us
  other arithmetic: 59.6 us -> 6.12 us
    reduce_scatter x5 -> x0, waiting for transfers between devices: 1170 us -> none  [apply_ham(): lax.psum_scatter(part_out, 'right', scatter_dimension=3, tiled=True)]
    psum x16 -> x0, blocking collectives: 1040 us -> none  [the longest x10 634 us: global_dots(): return lax.psum(local_dots, BOTH_AXES)]
    pallas_call x0 -> x1, Pallas kernels: none -> 351 us  [run_kernel(): pl.pallas_call(kernel, out_shape=(jax.ShapeDtypeStruct((NCH, HALF, WIDE),...]
    dot_general x15 -> x0, matrix products: 225 us -> none  [the longest x5 130 us: apply_ham(): jnp.einsum('alc,asub->lcsub', left_full, vec_full, precision=PREC_MODE, p...]
    all_gather x0 -> x1, waiting for transfers between devices: none -> 78.7 us  [local_fn(): lax.all_gather(jnp.transpose(env_right, (1, 0, 2)), ('ya', 'x'), axis=0,...]
    reduce_sum x16 -> x0, other arithmetic: 45 us -> none  [the longest x10 26.6 us: global_dots(): jnp.sum(basis_vec * residual)]
    all_to_all x1 -> x5, local copies, waits for them, and re-layouts: 37 us -> 1.38 us  [the longest x2 1.13 us: local_fn(): lax.all_to_all(swap_rows(psi_loc.reshape(768, 4, 24)), ('ya', 'x'), 0, 2,...]
    dot_general x5 -> x0, local copies, waits for them, and re-layouts: 33.5 us -> none  [apply_ham(): jnp.einsum('rtvcb,bre->tvce', stage_two, env_right, precision=PREC_MODE,...]
  transfers between devices with their start and end apart: 6 -> 3, of which waited for: 5 -> 3; matrix products, arithmetic and copies ran while one was open for 0% -> 6% of each run, Pallas kernels for 0% -> 0%
where the time goes in v2:
time: 506 us; the launch traced here: 505 us
  Pallas kernels  351 us (69%)
  waiting for transfers between devices  83.3 us (16%)
  local copies, waits for them, and re-layouts  40.9 us (8%)
  between operations  14.2 us (3%)
  starting transfers between devices  9.35 us (2%)
  other arithmetic  6.12 us (1%)
    pallas_call x1, Pallas kernels, run_kernel(): pl.pallas_call(kernel, out_shape=(jax.ShapeDtypeStruct((NCH, HALF, WIDE),...  351 us
    all_gather x1, waiting for transfers between devices, local_fn(): lax.all_gather(jnp.transpose(env_right, (1, 0, 2)), ('ya', 'x'), axis=0,...  78.7 us
    all_gather x1, local copies, waits for them, and re-layouts, local_fn(): lax.all_gather(jnp.transpose(env_right, (1, 0, 2)), ('ya', 'x'), axis=0,...  12.8 us
  transfers between devices with their start and end apart: 3, of which 3 were waited for; matrix products, arithmetic and copies ran while one was open for 6% of the time, Pallas kernels for 0%

profile of v2, /device:TPU:1, one launch (start us, length us, event | category | flops | bytes accessed | tf_op | source)
XLA Modules:
  0.0 504.7 jit_solution(1756896465958728392)
XLA Ops:
  7.2 0.0 copy-start
  7.2 0.0 all-gather.2.cloned.1.call-start
  7.2 0.7 all-gather.2.cloned.1.call-update
  7.9 2.4 copy.37
  10.4 0.0 copy-done
  10.4 0.7 copy.38
  11.1 1.3 broadcast_select_fusion
  12.5 0.0 copy-start.1
  12.5 4.2 reshape.54
  16.7 5.9 %all-to-all-start = ((f32[8,1,9216]{2,1,0:T(1,128)}), f32[8,1,9216]{2,1,0:T(1,128)S(1)}, u32[]{:S(2)}, u32[]{:S(2)}) async-start(f32[8,1,9216]{2,1,0:T(1,128)} %reshape.54), calls=%async_computation | async-start | bytes 589824 | tf_op jit(solution)/shard_map/all_to_all | solution.py:499
  22.5 0.0 copy-done.1
  22.5 0.1 copy.42
  22.6 2.7 multiply_bitcast_fusion
  25.3 4.7 reshape.48.mix_ref
  30.0 1.7 all-to-all-done
  31.6 0.5 broadcast.4
  32.1 1.3 reduce.2
  33.5 2.1 reshape.55
  35.6 0.6 copy.51
  36.2 0.5 reshape.45
  36.7 1.1 copy.41
  37.8 1.1 reshape.46.psi_ref
  38.9 78.7 %all-gather.2.cloned.1.call-done = f32[64,24,1536]{2,0,1:T(8,128)} async-done(((f32[8,24,1536]{2,0,1:T(8,128)}), f32[64,24,1536]{2,0,1:T(8,128)}) %all-gather.2.cloned.1.call-update) | async-done | bytes 9437200 | tf_op jit(solution)/shard_map/all_gather | solution.py:498
  117.6 12.8 %copy.43 = f32[64,24,1536]{2,1,0:T(8,128)} copy(f32[64,24,1536]{2,0,1:T(8,128)} %all-gather.2.cloned.1.call-done) | data formatting | bytes 18874368 | tf_op jit(solution)/shard_map/all_gather | solution.py:498
  130.4 350.8 %lanczos.1 = (f32[6,48,256]{2,1,0:T(8,128)}, f32[6,8,128]{2,1,0:T(8,128)}, f32[6,8,128]{2,1,0:T(8,128)}) custom-call(f32[6,48,256]{2,1,0:T(8,128)} %reshape.46.psi_ref, f32[256,256]{1,0:T(8,128)} %reshape.48.mix_ref, f32[6144,1536]{1,0:T(8,128)} %bitcast.44, f32[1536,1536]{1,0:T(8,128)} %bitcast.43), custom_call_target="tpu_custom_call" | custom-call | tf_op jit(solution)/shard_map/lanczos/pallas_call | solution.py:449
  481.2 1.2 reshape.51
  482.4 0.4 copy.53
  482.9 0.4 reshape.52
  483.3 0.9 copy.45
  484.2 3.5 all-to-all-start.1
  487.7 1.3 fusion.3
  489.0 3.8 stack.3
  492.8 1.4 slice_reduce_fusion
  494.1 2.3 all-to-all-done.1
  496.4 0.1 copy.49
  496.6 0.2 all_to_all.30
  496.7 0.1 copy.47
  496.8 0.1 concatenate.13
  496.9 0.1 copy.48
  497.0 0.1 concatenate.14
  497.1 0.7 maximum_select_fusion
  (5 shorter events, 0.1 us)
Async XLA Ops:
  7.2 3.2 copy-start
  7.2 110.4 %all-gather.2.cloned.1.call-start = ((), (), s32[]{:S(2)}) async-start(), calls=%async_computation.2 | async-start | bytes 10616832 | tf_op jit(solution)/shard_map/all_gather | solution.py:498
  12.5 10.1 %copy-start.1 = (f32[8,8,2,2,2,2]{1,5,4,3,2,0:T(2,128)S(1)}, f32[8,8,2,2,2,2]{1,5,4,3,2,0:T(2,128)}, u32[]{:S(2)}) copy-start(f32[8,8,2,2,2,2]{1,5,4,3,2,0:T(2,128)} %param.7) | copy-start | bytes 12292
  16.7 15.0 %all-to-all-start = ((f32[8,1,9216]{2,1,0:T(1,128)}), f32[8,1,9216]{2,1,0:T(1,128)S(1)}, u32[]{:S(2)}, u32[]{:S(2)}) async-start(f32[8,1,9216]{2,1,0:T(1,128)} %reshape.54), calls=%async_computation | async-start | bytes 589824 | tf_op jit(solution)/shard_map/all_to_all | solution.py:499
  484.2 12.2 %all-to-all-start.1 = ((f32[96,4,192]{0,1,2:T(4,128)}), f32[96,4,192]{0,1,2:T(4,128)S(1)}, u32[]{:S(2)}, u32[]{:S(2)}) async-start(f32[96,4,192]{0,1,2:T(4,128)} %copy.45), calls=%async_computation.1 | async-start | bytes 786432 | tf_op jit(solution)/shard_map/all_to_all | solution.py:505
Sparse Core Ops, SparseCore 0:
  9.6 107.9 all-gather.1

commit v3 on v2

v3 whole, which is shorter than its diff:
```python
import functools
import math

import jax
import jax.numpy as jnp
from jax import lax
from jax.experimental import pallas as pl
from jax.experimental.pallas import tpu as pltpu
from jax.sharding import Mesh
from jax.sharding import PartitionSpec as P

STEPS = 5
AXES = ("z", "yb", "ya", "x", "core")
F32, BF16 = jnp.float32, jnp.bfloat16
MESH = pl.DeviceIdType.MESH
D = 1536
HALF = 48
NCH = 6
LANE = 128
WIDE = 256
MROWS = 768


def split3(val):
    hi = val.astype(BF16)
    rest = val - hi.astype(F32)
    mid = rest.astype(BF16)
    low = (rest - mid.astype(F32)).astype(BF16)
    return hi, mid, low


def swap(val):
    return pltpu.roll(val, 64, axis=val.ndim - 1)


def low_half(shape):
    return lax.broadcasted_iota(jnp.int32, shape, len(shape) - 1) < 64


def dot(a, b):
    return jnp.dot(a, b, preferred_element_type=F32)


def dot6(a, b, k):
    return dot(a[...], b[...]) + dot(a[:, : 2 * k], b[k:, :]) + dot(a[:, :k], b[2 * k :, :])


BOTH, TRIO, QUAD = range(2), range(3), range(4)


def loop(n, body):
    def run(i, carry):
        body(i)
        return carry

    lax.fori_loop(0, n, run, 0)


def top(n):
    return pl.ds(0, n)


def mult(val, n):
    return pl.multiple_of(val, n)


def seg(i, size):
    return slice(i * size, (i + 1) * size)


def row1(i):
    return slice(i, i + 1)


def wide(val):
    return jnp.concatenate([val, val], axis=1)


def pair_halves(e, o):
    lo = low_half(e.shape)
    return jnp.where(lo, e, swap(o)), jnp.where(lo, swap(e), o)


def fold(val):
    return jnp.sum(val.reshape(-1, 8, LANE), axis=0)


def kernel(
    psi_ref, wsm_ref, el_ref, rt_ref, v_out, a_out, b_out,
    l3, r3, w3, gb, v3, t1, tq, t2, o3, sb, rsb, xs, vs, u1, stage, rbuf, pbuf, obuf, obr, dots, ra, rb, cg, gam, gram,
    rs_recv, rs_last, rs_send, ag_recv, ag_last, ag_send, fw_recv, fw_send, ra_recv, ra_send, rb_recv, rb_send,
    st_sem, rl_sem, rr_recv, rr_last, rr_send, rf_recv, rf_send, ps_recv, ps_send, ou_recv, ou_send,
):
    z, yb, ya, x, core = (lax.axis_index(name) for name in AXES)
    row = lax.rem(ya + yb, 2)
    ia8 = row * 4 + x
    ia = core * 8 + ia8
    ib = z * 2 + yb
    mem = ya * 4 + x

    def a_peer(d, other=False):
        to_row = lax.rem(row + d // 4, 2)
        return {"z": z, "yb": yb, "ya": lax.rem(to_row + yb, 2), "x": lax.rem(x + d % 4, 4), "core": 1 - core if other else core}

    def b_peer(d):
        to_yb = lax.rem(yb + d // 4, 2)
        return {"z": lax.rem(z + d % 4, 4), "yb": to_yb, "ya": lax.rem(row + to_yb, 2), "x": x, "core": core}

    partner = a_peer(0, True)
    a_peers = [a_peer(d) for d in range(1, 8)] + [a_peer(d, True) for d in range(8)]
    b_peers = [b_peer(d) for d in range(1, 8)]
    x_peers, ya_peer = a_peers[:3], a_peers[3]
    z_peers, yb_peer = b_peers[:3], b_peers[3]

    barrier = pltpu.get_barrier_semaphore()
    for peer in a_peers + b_peers:
        pl.semaphore_signal(barrier, inc=1, device_id=peer, device_id_type=MESH)
    pl.semaphore_wait(barrier, len(a_peers) + len(b_peers))

    def remote(src, dst, send, recv, peer):
        pltpu.make_async_remote_copy(src_ref=src, dst_ref=dst, send_sem=send, recv_sem=recv, device_id=peer, device_id_type=MESH).start()

    def wait_bytes(ref, sem):
        pltpu.make_async_copy(ref, ref, sem).wait()

    def blocks(k, n):
        return rsb.at[0, k, top(n)]

    def ag_first(par, k, h):
        mine = gb.at[par, k, ia]
        for peer in x_peers:
            remote(mine, mine, ag_send.at[k], (ag_recv if h else ag_last).at[par, k], peer)
        if not h:
            remote(mine, mine, ag_send.at[k], ag_recv.at[par, k], ya_peer)

    def ag_second(par, k, h):
        wait_bytes(blocks(k, 3 if h else 1), ag_recv.at[par, k])
        if h:
            part = gb.at[par, k, pl.ds(core * 8 + row * 4, 4)]
            remote(part, part, ag_send.at[k], ag_last.at[par, k], ya_peer)
        else:
            part = gb.at[par, k, core * 8 + (1 - row) * 4 + x]
            for peer in x_peers:
                remote(part, part, ag_send.at[k], ag_last.at[par, k], peer)

    def ag_forward(par, k, h, m):
        wait_bytes(blocks(k, 4 if h else 6), ag_last.at[par, k])

        @pl.when(m > 0)
        def _():
            wait_bytes(gb.at[0, k, top(8)], fw_send.at[k])

        part = gb.at[par, k, pl.ds(core * 8, 8)]
        remote(part, part, fw_send.at[k], fw_recv.at[par, k], partner)

    def rs_first(par, k, h):
        if h:
            remote(sb.at[k, pl.ds((1 - yb) * 4, 4)], rsb.at[par, k, top(4)], rs_send.at[k], rs_recv.at[par, k], yb_peer)
        else:
            for d, peer in enumerate(z_peers):
                src = sb.at[k, pl.ds(lax.rem(z + d + 1, 4) * 2, 2)]
                remote(src, rsb.at[par, k, pl.ds(2 * d, 2)], rs_send.at[k], rs_recv.at[par, k], peer)

    def rs_second(par, k, h):
        wait_bytes(blocks(k, 4 if h else 6), rs_recv.at[par, k])
        if h:
            for j in QUAD:
                sb[k, yb * 4 + j] = sb[k, yb * 4 + j] + rsb[par, k, j]
            for d, peer in enumerate(z_peers):
                src = sb.at[k, yb * 4 + lax.rem(z + d + 1, 4)]
                remote(src, rsb.at[par, k, 4 + d], rs_send.at[k], rs_last.at[par, k], peer)
        else:
            for j in BOTH:
                sb[k, z * 2 + j] = sb[k, z * 2 + j] + rsb[par, k, j] + rsb[par, k, 2 + j] + rsb[par, k, 4 + j]
            remote(sb.at[k, z * 2 + 1 - yb], rsb.at[par, k, 6], rs_send.at[k], rs_last.at[par, k], yb_peer)

    def combine(m, k, h):
        prev = lax.rem(m + 1, 2)
        wait_bytes(blocks(k, 3 if h else 1), rs_last.at[prev, k])
        if h:
            w = sb[k, yb * 4 + z] + rsb[prev, k, 4] + rsb[prev, k, 5] + rsb[prev, k, 6]
        else:
            w = sb[k, ib] + rsb[prev, k, 6]
        for i in range(STEPS):
            w = w - wide(gam[row1(i), :]) * xs[i + 1, k]
        w = w * wide(gam[row1(STEPS), :])
        xs[m, k] = w
        local_dots(m, k, w)

    def publish(m, k, h, first):
        par = lax.rem(m, 2)
        if not first:
            wait_bytes(blocks(k, 7), ag_send.at[k])
        gb[par, k, ia] = xs[m, k]
        ag_first(par, k, h)

    def local_dots(m, k, cur):
        new = vs[jnp.maximum(m - 1, 0), k]
        for i in range(STEPS):
            vec = vs[i, k]
            dots[i] = dots[i] + fold(vec * cur)
            dots[5 + i] = dots[5 + i] + fold(vec * new)

    def red_rows(which, pairs):
        ra[which, ia] = jnp.zeros((16, LANE), F32)
        for src, dst in pairs:
            ra[which, ia, row1(dst), :] = jnp.sum(dots[src], axis=0, keepdims=True)
        mine = ra.at[which, ia]
        for peer in a_peers:
            remote(mine, mine, ra_send.at[which], ra_recv.at[which], peer)
        dots[...] = jnp.zeros_like(dots)

    def red_mid(which):
        wait_bytes(ra.at[which, top(15)], ra_recv.at[which])
        wait_bytes(ra.at[which, top(15)], ra_send.at[which])
        total = ra[which, 0]
        for i in range(1, 16):
            total = total + ra[which, i]
        rb[which, ib] = total
        mine = rb.at[which, ib]
        for peer in b_peers:
            remote(mine, mine, rb_send.at[which], rb_recv.at[which], peer)

    def red_end(which):
        wait_bytes(rb.at[which, top(7)], rb_recv.at[which])
        wait_bytes(rb.at[which, top(7)], rb_send.at[which])
        total = rb[which, 0]
        for i in range(1, 8):
            total = total + rb[which, i]
        return jnp.broadcast_to(jnp.sum(total, axis=1, keepdims=True), (16, LANE))

    def red1_start():
        red_rows(0, [(i, i) for i in range(5)] + [(5 + i, 8 + i) for i in range(5)])

    def red1_end(m):
        total = red_end(0)
        cg[...] = total[0:8]
        gram[jnp.maximum(m - 1, 0)] = total[8:16]
        a_out[m] = total[0:8]

        def piece(k):
            cur = xs[m, k]
            for i in range(STEPS):
                cur = cur - wide(cg[row1(i), :]) * vs[i, k]
            u1[k] = cur
            for i in range(STEPS):
                dots[i] = dots[i] + fold(vs[i, k] * cur)
            dots[5] = dots[5] + fold(cur * cur)

        loop(NCH, piece)
        red_rows(1, [(i, i) for i in range(5)] + [(5, 8)])

    def red2_end(m, last):
        total = red_end(1)
        d8 = total[0:8]
        sq = total[8:9]
        for i in range(STEPS):
            di = d8[row1(i)]
            inner = jnp.sum(d8 * gram[i], axis=0, keepdims=True)
            sq = sq - 2.0 * di * di + di * (2.0 * inner - di * gram[i, row1(i), :])
        beta = jnp.sqrt(sq)
        inv = 1.0 / beta
        b_out[m] = jnp.broadcast_to(beta, (8, LANE))
        gam[...] = cg[...] + d8
        gam[row1(STEPS), :] = inv
        scale = wide(inv * math.sqrt(float(4 * D * D)) if last else inv)

        def piece(k):
            cur = u1[k]
            for i in range(STEPS):
                cur = cur - wide(d8[row1(i)]) * vs[i, k]
            if last:
                u1[k] = cur * scale
            else:
                vs[m, k] = cur * scale

        loop(NCH, piece)

    def split_chunk(par, n):
        def piece(i):
            for h in BOTH:
                r = mult(i * 96 + h * HALF, 16)
                for part, val in enumerate(reversed(split3(gb[par, 2 * n + h, i]))):
                    v3[pl.ds(part * D + r, HALF), :] = val

        loop(16, piece)

    def mix_chunk(n):
        def quad(q):
            r0 = mult(q * 256, 256)
            xg = [t1[pl.ds(r0 + 64 * i, 64), :] for i in QUAD]
            for p in BOTH:
                for sp in BOTH:
                    e, o = (xg[2 * p + i][:, seg(sp, LANE)] for i in BOTH)
                    for s, val in enumerate(pair_halves(e, o)):
                        for part, piece in enumerate(reversed(split3(val))):
                            tq[seg(4 * part + 2 * sp + s, 64), seg(p, LANE)] = piece
            out = dot6(w3, tq, WIDE)
            for p in BOTH:
                pp = 2 * q + p
                h = pp // 3
                base = h * 192 + (pp - 3 * h) * 16
                for t in QUAD:
                    r = mult(base + t * HALF, 16)
                    for rp in QUAD:
                        e, f = (out[seg(8 * t + 2 * rp + i, 8), seg(p, LANE)] for i in BOTH)
                        g = jnp.concatenate(pair_halves(e, f), axis=0)
                        for part, val in enumerate(split3(g)):
                            t2[pl.ds(r, 16), pl.ds(mult(part * D + n * 512 + rp * LANE, LANE), LANE)] = val

        loop(3, quad)

    def out_chunk(m, n, h):
        k = 2 * n + h
        o3[...] = dot6(t2.at[seg(h, 192)], r3.at[:, pl.ds(mult(n * 512, 512), 512)], D)

        @pl.when(m > 0)
        def _():
            wait_bytes(blocks(k, 7), rs_send.at[k])

        for j in QUAD:
            y = [o3[seg(t, HALF), seg(j, LANE)] for t in QUAD]
            for sp in BOTH:
                for i, val in enumerate(pair_halves(y[2 * sp], y[2 * sp + 1])):
                    sb[k, 4 * i + j if h else 2 * j + i, :, seg(sp, LANE)] = val
        rs_first(lax.rem(m, 2), k, h)

    def rg_first(p):
        r = core * 4 + p
        mine = rbuf.at[r, mem]
        for peer in x_peers:
            remote(mine, mine, rr_send.at[p], (rr_recv if p % 2 else rr_last).at[p], peer)
        if p % 2 == 0:
            remote(mine, mine, rr_send.at[p], rr_recv.at[p], ya_peer)

    def rg_second(p):
        r = core * 4 + p
        wait_bytes(rbuf.at[0, top(3 if p % 2 else 1)], rr_recv.at[p])
        if p % 2:
            part = rbuf.at[r, pl.ds(ya * 4, 4)]
            remote(part, part, rr_send.at[p], rr_last.at[p], ya_peer)
        else:
            part = rbuf.at[r, (1 - ya) * 4 + x]
            for peer in x_peers:
                remote(part, part, rr_send.at[p], rr_last.at[p], peer)

    def rg_forward(p):
        wait_bytes(rbuf.at[0, top(4 if p % 2 else 6)], rr_last.at[p])
        part = rbuf.at[core * 4 + p]
        remote(part, part, rf_send.at[p], rf_recv.at[p], partner)

    def rg_split(r):
        def piece(mp):
            for g in TRIO:
                bg = 3 * mp + g
                n = bg // 4
                dst = mult(n * 512 + r * 64 + (bg - 4 * n) * 16, 16)
                for j in QUAD:
                    tl = []
                    for c in TRIO:
                        eights = [rbuf[r, 2 * mp + (2 * g + e) // 3, seg((2 * g + e) % 3, 8), seg(3 * j + c, LANE)] for e in BOTH]
                        tl.append(jnp.concatenate(eights, axis=0))
                    lo = low_half(tl[0].shape)
                    new = (jnp.where(lo, tl[0], tl[1]), swap(jnp.where(lo, tl[2], tl[0])), jnp.where(lo, tl[1], tl[2]))
                    for c in TRIO:
                        for part, val in enumerate(reversed(split3(new[c]))):
                            r3[pl.ds(part * D + dst, 16), seg(4 * c + j, LANE)] = val

        loop(4, piece)

    for d, peer in enumerate(a_peers[:7]):
        to = lax.rem(row + (d + 1) // 4, 2) * 4 + lax.rem(x + (d + 1) % 4, 4)
        remote(psi_ref.at[to], pbuf.at[mem], ps_send, ps_recv, peer)
    pbuf[mem] = psi_ref[ia8]

    def rt_copy(p):
        r = core * 4 + p
        return pltpu.make_async_copy(rt_ref.at[pl.ds(mult(r * 24, 24), 24)], rbuf.at[r, mem], rl_sem.at[p])

    for p in QUAD:
        rt_copy(p).start()

    def el_copy(i, slot):
        return pltpu.make_async_copy(el_ref.at[pl.ds(mult(ia8 * 768 + i * HALF, HALF), HALF)], stage.at[slot], st_sem.at[slot])

    el_copy(0, 0).start()

    def init(k):
        for i in range(STEPS):
            xs[i + 1, k] = jnp.zeros((HALF, WIDE), F32)
            vs[i, k] = jnp.zeros((HALF, WIDE), F32)

    loop(NCH, init)
    dots[...] = jnp.zeros_like(dots)
    gram[...] = jnp.zeros_like(gram)
    gam[...] = jnp.zeros_like(gam)

    i0 = lax.broadcasted_iota(jnp.int32, (WIDE, WIDE), 0)
    i1 = lax.broadcasted_iota(jnp.int32, (WIDE, WIDE), 1)
    same = (i0 & 7) == ((i1 >> 3) & 7)
    left = ((lax.broadcasted_iota(jnp.int32, (WIDE, 32), 0) >> 3) == lax.broadcasted_iota(jnp.int32, (WIDE, 32), 1)).astype(BF16)
    c1 = lax.broadcasted_iota(jnp.int32, (32, WIDE), 1)
    right = (((c1 >> 6) * 8 + (c1 & 7)) == lax.broadcasted_iota(jnp.int32, (32, WIDE), 0)).astype(BF16)
    for part, val in enumerate(split3(wsm_ref[...])):
        full = dot(dot(left, val).astype(BF16), right)
        w3[:, seg(part, WIDE)] = jnp.where(same, full, 0.0).astype(BF16)

    wait_bytes(pbuf.at[top(7)], ps_recv)
    for i in range(8):
        for s in QUAD:
            t1[s * 192 + i * 24 : s * 192 + i * 24 + 24, 0:LANE] = pbuf[i, seg(s, 24), :]
    for n in TRIO:
        for sp in BOTH:
            tile = jnp.concatenate([t1[seg(6 * sp + 3 * i + n, 64), 0:LANE] for i in BOTH], axis=0).T
            for h in BOTH:
                xs[0, 2 * n + h, :, seg(sp, LANE)] = tile[seg(h, HALF), :]
    for k in range(NCH):
        publish(0, k, k % 2, True)
    for p in QUAD:
        rt_copy(p).wait()
        rg_first(p)

    def first_dots(k):
        local_dots(0, k, xs[0, k])

    loop(NCH, first_dots)

    def el_piece(i):
        slot = lax.rem(i, 2)

        @pl.when(i < 15)
        def _():
            el_copy(i + 1, 1 - slot).start()

        el_copy(i, slot).wait()
        for c in range(6):
            for part, val in enumerate(split3(stage[slot, :, seg(c, WIDE)])):
                l3[pl.ds(mult(i * HALF, 16), HALF), seg(6 * part + c, WIDE)] = val

    loop(16, el_piece)
    for k in QUAD:
        ag_second(0, k, k % 2)

    def step(m):
        par = lax.rem(m, 2)
        red1_start()
        for h in BOTH:
            ag_forward(par, h, h, m)

        def chunk(n):
            for h in BOTH:
                wait_bytes(gb.at[par, 2 * n + h, pl.ds((1 - core) * 8, 8)], fw_recv.at[par, 2 * n + h])
            split_chunk(par, n)
            t1[...] = dot6(l3, v3, D)

            @pl.when(n == 0)
            def _():
                for h in BOTH:
                    ag_second(par, 4 + h, h)
                for h in BOTH:
                    ag_forward(par, 2 + h, h, m)
                red_mid(0)

                @pl.when(m == 0)
                def _():
                    for p in QUAD:
                        rg_second(p)

            @pl.when(n == 1)
            def _():
                for h in BOTH:
                    ag_forward(par, 4 + h, h, m)
                red1_end(m)

            mix_chunk(n)

            @pl.when(n == 2)
            def _():
                red_mid(1)


        loop(3, chunk)

        @pl.when(m == 0)
        def _():
            for p in QUAD:
                rg_forward(p)
            for p in QUAD:
                rg_split(core * 4 + p)
            for p in QUAD:
                wait_bytes(rbuf.at[0], rf_recv.at[p])
                rg_split((1 - core) * 4 + p)

        def outs(n):
            for h in BOTH:
                out_chunk(m, n, h)

                @pl.when(n > 0)
                def _():
                    rs_second(par, 2 * n - 2 + h, h)

            @pl.when(n == 1)
            def _():
                red2_end(m, False)


        loop(3, outs)
        more = m < STEPS - 1

        def finish(k):
            combine(m + 1, k, k % 2)

            @pl.when(more)
            def _():
                publish(m + 1, k, k % 2, False)

        def spread(k):
            @pl.when(more)
            def _():
                ag_second(1 - par, k, k % 2)

        for h in BOTH:
            finish(h)
        for h in BOTH:
            rs_second(par, 4 + h, h)
        for h in BOTH:
            finish(2 + h)
        for h in BOTH:
            spread(h)
        for h in BOTH:
            finish(4 + h)
        for h in BOTH:
            spread(2 + h)

    loop(STEPS, step)

    red1_start()
    red_mid(0)
    red1_end(STEPS)
    red_mid(1)
    red2_end(STEPS, True)
    for n in TRIO:
        for sp in BOTH:
            rows = [u1[2 * n + h, :, seg(sp, LANE)] for h in BOTH] + [jnp.zeros((32, LANE), F32)]
            tile = jnp.concatenate(rows, axis=0).T
            for s in BOTH:
                for g in range(8):
                    bg = 8 * n + g
                    obuf[bg // 3, seg((2 * sp + s) * 3 + bg % 3, 8), :] = tile[seg(8 * s + g, 8), :]
    for d, peer in enumerate(a_peers[:7]):
        to_row = lax.rem(row + (d + 1) // 4, 2)
        to = lax.rem(to_row + yb, 2) * 4 + lax.rem(x + (d + 1) % 4, 4)
        remote(obuf.at[to], obr.at[ia8], ou_send, ou_recv, peer)
    obr[ia8] = obuf[mem]
    for k in range(NCH):
        wait_bytes(blocks(k, 7), ag_send.at[k])
        wait_bytes(blocks(k, 7), rs_send.at[k])
        wait_bytes(gb.at[0, k, top(8)], fw_send.at[k])
    for p in QUAD:
        wait_bytes(rbuf.at[0, top(7)], rr_send.at[p])
        wait_bytes(rbuf.at[0], rf_send.at[p])
    wait_bytes(pbuf.at[top(7)], ps_send)
    wait_bytes(obr.at[top(7)], ou_recv)
    wait_bytes(obr.at[top(7)], ou_send)
    v_out[...] = obr[...]


def run_kernel(psi, wsm, el, rt):
    vmem = pl.BlockSpec(memory_space=pltpu.VMEM)
    hbm = pl.BlockSpec(memory_space=pl.ANY)
    dma = pltpu.SemaphoreType.DMA
    return pl.pallas_call(
        kernel,
        out_shape=(
            jax.ShapeDtypeStruct((8, 96, LANE), F32),
            jax.ShapeDtypeStruct((STEPS + 1, 8, LANE), F32),
            jax.ShapeDtypeStruct((STEPS + 1, 8, LANE), F32),
        ),
        in_specs=[vmem, vmem, hbm, hbm],
        out_specs=(vmem, vmem, vmem),
        scratch_shapes=[
            pltpu.VMEM((MROWS, 3 * D), BF16),
            pltpu.VMEM((3 * D, D), BF16),
            pltpu.VMEM((WIDE, MROWS), BF16),
            pltpu.VMEM((2, NCH, 16, HALF, WIDE), F32),
            pltpu.VMEM((3 * D, WIDE), BF16),
            pltpu.VMEM((MROWS, WIDE), F32),
            pltpu.VMEM((MROWS, WIDE), BF16),
            pltpu.VMEM((384, 3 * D), BF16),
            pltpu.VMEM((192, 512), F32),
            pltpu.VMEM((NCH, 8, HALF, WIDE), F32),
            pltpu.VMEM((2, NCH, 7, HALF, WIDE), F32),
            pltpu.VMEM((STEPS + 1, NCH, HALF, WIDE), F32),
            pltpu.VMEM((STEPS, NCH, HALF, WIDE), F32),
            pltpu.VMEM((NCH, HALF, WIDE), F32),
            pltpu.VMEM((2, HALF, D), F32),
            pltpu.VMEM((8, 8, 24, D), F32),
            pltpu.VMEM((8, 96, LANE), F32),
            pltpu.VMEM((8, 96, LANE), F32),
            pltpu.VMEM((8, 96, LANE), F32),
            pltpu.VMEM((10, 8, LANE), F32),
            pltpu.VMEM((2, 16, 16, LANE), F32),
            pltpu.VMEM((2, 8, 16, LANE), F32),
            pltpu.VMEM((8, LANE), F32),
            pltpu.VMEM((8, LANE), F32),
            pltpu.VMEM((STEPS, 8, LANE), F32),
            dma((2, NCH)), dma((2, NCH)), dma((NCH,)), dma((2, NCH)), dma((2, NCH)), dma((NCH,)), dma((2, NCH)), dma((NCH,)),
            dma((2,)), dma((2,)), dma((2,)), dma((2,)),
            dma((2,)), dma((4,)), dma((4,)), dma((4,)), dma((4,)), dma((4,)), dma((4,)), dma, dma, dma, dma,
        ],
        compiler_params=pltpu.CompilerParams(collective_id=0, has_side_effects=True, vmem_limit_bytes=67043328),
        name="lanczos",
    )(psi, wsm, el, rt)


def solution(mesh):
    grid = Mesh(mesh.devices.reshape(4, 2, 2, 4, 2), AXES)
    psi_spec = P("core", None, None, ("z", "yb", "ya", "x"))

    def local_fn(psi_loc, env_left, env_right, mpo_pair):
        rt = jnp.transpose(env_right, (1, 0, 2)).reshape(192, D)
        psi = jnp.transpose(psi_loc.reshape(8, 96, 96), (0, 2, 1))
        psi = jnp.pad(psi, ((0, 0), (0, 0), (0, 32)))
        wsm = jnp.transpose(mpo_pair.reshape(8, 8, 4, 4), (3, 1, 2, 0)).reshape(32, 32)
        vec, aa, bb = run_kernel(psi, wsm, env_left.reshape(6144, D), rt)
        out = jnp.transpose(vec[:, :, :96], (0, 2, 1)).reshape(psi_loc.shape)
        alpha = jnp.stack([aa[i + 1, i, 0] for i in range(STEPS)])
        return alpha, bb[1:, 0, 0], out

    return jax.shard_map(
        local_fn,
        mesh=grid,
        in_specs=(psi_spec, P("core", None, None), P(("z", "yb", "ya", "x"), None, None), P()),
        out_specs=(P(), P(), psi_spec),
        check_vma=False,
    )
```

time: 506 us -> 393 us (0.78)
  waiting for transfers between devices: 83.3 us -> 0 us
  local copies, waits for them, and re-layouts: 40.9 us -> 13.9 us
  Pallas kernels: 351 us -> 377 us
  between operations: 14.2 us -> 0.66 us
  starting transfers between devices: 9.35 us -> 0 us
  other arithmetic: 6.12 us -> 0 us
    all_gather x1 -> x0, waiting for transfers between devices: 78.7 us -> none  [local_fn(): lax.all_gather(jnp.transpose(env_right, (1, 0, 2)), ('ya', 'x'), axis=0,...]
    pallas_call x1, Pallas kernels: 351 us -> 377 us  [run_kernel(): pl.pallas_call(kernel, out_shape=(jax.ShapeDtypeStruct((8, 96, LANE), F32...]
    all_gather x1 -> x0, local copies, waits for them, and re-layouts: 12.8 us -> none  [local_fn(): lax.all_gather(jnp.transpose(env_right, (1, 0, 2)), ('ya', 'x'), axis=0,...]
    all_to_all x2 -> x0, starting transfers between devices: 9.31 us -> none  [the longest x1 5.86 us: local_fn(): lax.all_to_all(swap_rows(psi_loc.reshape(768, 4, 24)), ('ya', 'x'), 0, 2,...]
    unnamed x7 -> x2, local copies, waits for them, and re-layouts: 8.74 us -> 0.01 us
    reshape x8 -> x5, local copies, waits for them, and re-layouts: 9.32 us -> 3.74 us  [the longest x2 1.22 us: local_fn(): psi = jnp.transpose(psi_loc.reshape(8, 96, 96), (0, 2, 1))]
  transfers between devices with their start and end apart: 3 -> 0, of which waited for: 3 -> 0; matrix products, arithmetic and copies ran while one was open for 6% -> 0% of each run, Pallas kernels for 0% -> 0%
where the time goes in v3:
time: 393 us; the launch traced here: 392 us
  Pallas kernels  377 us (96%)
  local copies, waits for them, and re-layouts  13.9 us (4%)
    pallas_call x1, Pallas kernels, run_kernel(): pl.pallas_call(kernel, out_shape=(jax.ShapeDtypeStruct((8, 96, LANE), F32...  377 us

profile of v3, /device:TPU:1, one launch (start us, length us, event | category | flops | bytes accessed | tf_op | source)
XLA Modules:
  0.0 391.8 jit_solution(13027011909425279122)
XLA Ops:
  0.6 0.9 copy.10
  1.6 0.0 copy-start
  1.6 0.7 reshape.26.wsm_ref
  2.3 1.1 reshape.24
  3.4 0.1 copy.14
  3.5 0.8 pad.4.psi_ref
  4.3 0.0 copy-done
  4.3 1.7 copy.11
  6.0 377.2 %lanczos.1 = (f32[8,96,128]{2,1,0:T(8,128)}, f32[6,8,128]{2,1,0:T(8,128)}, f32[6,8,128]{2,1,0:T(8,128)}) custom-call(f32[8,96,128]{2,1,0:T(8,128)} %pad.4.psi_ref, f32[32,32]{1,0:T(8,128)} %reshape.26.wsm_ref, f32[6144,1536]{1,0:T(8,128)} %bitcast.21, f32[192,1536]{1,0:T(8,128)} %bitcast.22), custom_call_target="tpu_custom_call" | custom-call | tf_op jit(solution)/shard_map/lanczos/pallas_call | solution.py:572
  383.2 1.3 fusion
  384.5 3.8 stack.3
  388.3 1.4 slice_reduce_fusion
  389.6 1.0 slice_bitcast_fusion
  390.6 0.2 copy.12
  390.9 0.9 reshape.29
Async XLA Ops:
  1.6 2.7 copy-start

commit v4 on v3

v4 whole, which is shorter than its diff:
```python
import functools
import math

import jax
import jax.numpy as jnp
from jax import lax
from jax.experimental import pallas as pl
from jax.experimental.pallas import tpu as pltpu
from jax.sharding import Mesh
from jax.sharding import PartitionSpec as P

STEPS = 5
AXES = ("z", "yb", "ya", "x", "core")
F32, BF16 = jnp.float32, jnp.bfloat16
MESH = pl.DeviceIdType.MESH
D = 1536
HALF = 48
NCH = 6
LANE = 128
WIDE = 256
MROWS = 768
PART = 24
THIRD = 512
LAST = STEPS - 1


def split3(val):
    hi = val.astype(BF16)
    rest = val - hi.astype(F32)
    mid = rest.astype(BF16)
    low = (rest - mid.astype(F32)).astype(BF16)
    return hi, mid, low


def swap(val):
    return pltpu.roll(val, 64, axis=val.ndim - 1)


def low_half(shape):
    return lax.broadcasted_iota(jnp.int32, shape, len(shape) - 1) < 64


def dot(a, b):
    return jnp.dot(a, b, preferred_element_type=F32)


def dot6(a, b, k):
    return dot(a[...], b[...]) + dot(a[:, : 2 * k], b[k:, :]) + dot(a[:, :k], b[2 * k :, :])


BOTH, TRIO, QUAD = range(2), range(3), range(4)


def loop(n, body):
    def run(i, carry):
        body(i)
        return carry

    lax.fori_loop(0, n, run, 0)


def top(n):
    return pl.ds(0, n)


def mult(val, n):
    return pl.multiple_of(val, n)


def seg(i, size):
    return slice(i * size, (i + 1) * size)


def row1(i):
    return slice(i, i + 1)


def wide(val):
    return jnp.concatenate([val, val], axis=1)


def pair_halves(e, o):
    lo = low_half(e.shape)
    return jnp.where(lo, e, swap(o)), jnp.where(lo, swap(e), o)


def fold(val):
    return jnp.sum(val.reshape(-1, 8, LANE), axis=0)


def kernel(
    psi_ref, wsm_ref, el_ref, rt_ref, v_out, ab_out,
    l3, r3, w3, gb, v3, t1, tq, t2, o3, sz, sy, rsb, xs, vs, u1, stage, rbuf, pbuf, obuf, obr, dots, ra, rb, cg, gam, gram,
    rs_first, rs_last, rs_send, ag_first, ag_last, ag_send, fw_recv, fw_send, ra_recv, ra_send, rb_recv, rb_send,
    st_sem, rr_first, rr_last, rr_send, rf_recv, rf_send, ps_recv, ps_send, ou_recv, ou_send,
):
    z, yb, ya, x, core = (lax.axis_index(name) for name in AXES)
    row = lax.rem(ya + yb, 2)
    ia8 = row * 4 + x
    ia = core * 8 + ia8
    ib = z * 2 + yb
    mem = ya * 4 + x

    def a_peer(d, other=False):
        to_row = lax.rem(row + d // 4, 2)
        return {"z": z, "yb": yb, "ya": lax.rem(to_row + yb, 2), "x": lax.rem(x + d % 4, 4), "core": 1 - core if other else core}

    def b_peer(d):
        to_yb = lax.rem(yb + d // 4, 2)
        return {"z": lax.rem(z + d % 4, 4), "yb": to_yb, "ya": lax.rem(row + to_yb, 2), "x": x, "core": core}

    partner = a_peer(0, True)
    a_peers = [a_peer(d) for d in range(1, 8)] + [a_peer(d, True) for d in range(8)]
    b_peers = [b_peer(d) for d in range(1, 8)]
    x_peers, ya_peer = a_peers[:3], a_peers[3]
    z_peers, yb_peer = b_peers[:3], b_peers[3]

    barrier = pltpu.get_barrier_semaphore()
    for peer in a_peers + b_peers:
        pl.semaphore_signal(barrier, inc=1, device_id=peer, device_id_type=MESH)
    pl.semaphore_wait(barrier, len(a_peers) + len(b_peers))

    def remote(src, dst, send, recv, peer):
        pltpu.make_async_remote_copy(src_ref=src, dst_ref=dst, send_sem=send, recv_sem=recv, device_id=peer, device_id_type=MESH).start()

    def wait_bytes(ref, sem):
        pltpu.make_async_copy(ref, ref, sem).wait()

    def parts(k, n):
        return rsb.at[0, k, top(n)]

    upper, lower = top(PART), pl.ds(PART, PART)

    def publish(m, k, first):
        par = lax.rem(m, 2)
        if not first:
            wait_bytes(parts(k, 14), ag_send.at[k])
        gb[par, k, ia] = xs[m, k]
        low, up = gb.at[par, k, ia, lower], gb.at[par, k, ia, upper]
        for peer in x_peers:
            remote(low, low, ag_send.at[k], ag_first.at[par, k], peer)
        remote(up, up, ag_send.at[k], ag_first.at[par, k], ya_peer)
        for peer in x_peers:
            remote(up, up, ag_send.at[k], ag_last.at[par, k], peer)

    def ag_second(par, k):
        wait_bytes(parts(k, 4), ag_first.at[par, k])
        low = gb.at[par, k, pl.ds(core * 8 + row * 4, 4), lower]
        remote(low, low, ag_send.at[k], ag_last.at[par, k], ya_peer)
        up = gb.at[par, k, core * 8 + (1 - row) * 4 + x, upper]
        for peer in x_peers:
            remote(up, up, ag_send.at[k], ag_last.at[par, k], peer)

    def ag_forward(par, k, m):
        wait_bytes(parts(k, 10), ag_last.at[par, k])

        @pl.when(m > 0)
        def _():
            wait_bytes(gb.at[0, k, top(8)], fw_send.at[k])

        part = gb.at[par, k, pl.ds(core * 8, 8)]
        remote(part, part, fw_send.at[k], fw_recv.at[par, k], partner)

    def rs_start(par, k):
        remote(sy.at[k, 1 - yb], rsb.at[par, k, pl.ds(6, 4)], rs_send.at[k], rs_first.at[par, k], yb_peer)
        for d, peer in enumerate(z_peers):
            remote(sz.at[k, lax.rem(z + d + 1, 4)], rsb.at[par, k, pl.ds(2 * d, 2)], rs_send.at[k], rs_first.at[par, k], peer)

    def rs_second(par, k):
        wait_bytes(parts(k, 10), rs_first.at[par, k])
        for j in QUAD:
            sy[k, yb, j] = sy[k, yb, j] + rsb[par, k, 6 + j]
        for d, peer in enumerate(z_peers):
            remote(sy.at[k, yb, lax.rem(z + d + 1, 4)], rsb.at[par, k, 11 + d], rs_send.at[k], rs_last.at[par, k], peer)
        for j in BOTH:
            sz[k, z, j] = sz[k, z, j] + rsb[par, k, j] + rsb[par, k, 2 + j] + rsb[par, k, 4 + j]
        remote(sz.at[k, z, 1 - yb], rsb.at[par, k, 10], rs_send.at[k], rs_last.at[par, k], yb_peer)

    def combine(m, k):
        prev = lax.rem(m + 1, 2)
        wait_bytes(parts(k, 4), rs_last.at[prev, k])
        up = sz[k, z, yb] + rsb[prev, k, 10]
        low = sy[k, yb, z] + rsb[prev, k, 11] + rsb[prev, k, 12] + rsb[prev, k, 13]
        w = jnp.concatenate([up, low], axis=0)
        for i in range(STEPS):
            w = w - wide(gam[row1(i), :]) * xs[i + 1, k]
        w = w * wide(gam[row1(STEPS), :])
        xs[m, k] = w
        local_dots(m, k, w)

    def local_dots(m, k, cur):
        new = vs[jnp.maximum(m - 1, 0), k]
        for i in range(STEPS):
            vec = vs[i, k]
            dots[i] = dots[i] + fold(vec * cur)
            dots[STEPS + i] = dots[STEPS + i] + fold(vec * new)

    def red_rows(which, pairs):
        ra[which, ia] = jnp.zeros((16, LANE), F32)
        for src, dst in pairs:
            ra[which, ia, row1(dst), :] = jnp.sum(dots[src], axis=0, keepdims=True)
        mine = ra.at[which, ia]
        for peer in a_peers:
            remote(mine, mine, ra_send.at[which], ra_recv.at[which], peer)
        dots[...] = jnp.zeros_like(dots)

    def red_mid(which):
        wait_bytes(ra.at[which, top(15)], ra_recv.at[which])
        wait_bytes(ra.at[which, top(15)], ra_send.at[which])
        total = ra[which, 0]
        for i in range(1, 16):
            total = total + ra[which, i]
        rb[which, ib] = total
        mine = rb.at[which, ib]
        for peer in b_peers:
            remote(mine, mine, rb_send.at[which], rb_recv.at[which], peer)

    def red_end(which):
        wait_bytes(rb.at[which, top(7)], rb_recv.at[which])
        wait_bytes(rb.at[which, top(7)], rb_send.at[which])
        total = rb[which, 0]
        for i in range(1, 8):
            total = total + rb[which, i]
        return jnp.broadcast_to(jnp.sum(total, axis=1, keepdims=True), (16, LANE))

    def record(line, m, val):
        here = lax.broadcasted_iota(jnp.int32, (1, LANE), 1) == m - 1
        ab_out[row1(line), :] = jnp.where(here, val, ab_out[row1(line), :])

    def red1_start():
        red_rows(0, [(i, i) for i in range(STEPS)] + [(STEPS + i, 8 + i) for i in range(STEPS)])

    def red1_end(m):
        total = red_end(0)
        c8 = total[:8]
        cg[...] = c8
        gram[jnp.maximum(m - 1, 0)] = total[8:]
        now = lax.broadcasted_iota(jnp.int32, c8.shape, 0) == m - 1
        record(0, m, jnp.sum(jnp.where(now, c8, 0.0), axis=0, keepdims=True))

        def piece(k):
            cur = xs[m, k]
            for i in range(STEPS):
                cur = cur - wide(cg[row1(i), :]) * vs[i, k]
            u1[k] = cur
            for i in range(STEPS):
                dots[i] = dots[i] + fold(vs[i, k] * cur)
            dots[STEPS] = dots[STEPS] + fold(cur * cur)

        loop(NCH, piece)
        red_rows(1, [(i, i) for i in range(STEPS)] + [(STEPS, 8)])

    def red2_end(m, last):
        total = red_end(1)
        d8 = total[:8]
        sq = total[8:9]
        for i in range(STEPS):
            di = d8[row1(i)]
            inner = jnp.sum(d8 * gram[i], axis=0, keepdims=True)
            sq = sq - 2.0 * di * di + di * (2.0 * inner - di * gram[i, row1(i), :])
        beta = jnp.sqrt(sq)
        inv = 1.0 / beta
        record(1, m, beta)
        gam[...] = cg[...] + d8
        gam[row1(STEPS), :] = inv
        scale = wide(inv * math.sqrt(float(4 * D * D)) if last else inv)

        def piece(k):
            cur = u1[k]
            for i in range(STEPS):
                cur = cur - wide(d8[row1(i)]) * vs[i, k]
            if last:
                u1[k] = cur * scale
            else:
                vs[m, k] = cur * scale

        loop(NCH, piece)

    def left_half(par, k):
        wait_bytes(gb.at[par, k, pl.ds((1 - core) * 8, 8)], fw_recv.at[par, k])
        h = lax.rem(k, 2)
        base = mult(3 * MROWS * h, 3 * MROWS)

        def piece(i):
            for part, val in enumerate(reversed(split3(gb[par, k, i]))):
                v3[pl.ds(mult(base + part * MROWS + i * HALF, 16), HALF), :] = val

        loop(16, piece)
        val = dot6(l3.at[:, pl.ds(base, 3 * MROWS)], v3.at[pl.ds(base, 3 * MROWS)], MROWS)
        t1[...] = jnp.where(h == 0, 0.0, t1[...]) + val

    def mix_chunk(n):
        for q in TRIO:
            xg = [t1[seg(4 * q + i, 64), :] for i in QUAD]
            for p in BOTH:
                for sp in BOTH:
                    e, o = (xg[2 * p + i][:, seg(sp, LANE)] for i in BOTH)
                    for s, val in enumerate(pair_halves(e, o)):
                        for part, piece in enumerate(reversed(split3(val))):
                            tq[seg(4 * part + 2 * sp + s, 64), seg(2 * q + p, LANE)] = piece
        out = dot6(w3, tq, WIDE)
        for pp in range(NCH):
            h, g3 = divmod(pp, 3)
            for t in QUAD:
                for rp in QUAD:
                    e, f = (out[seg(8 * t + 2 * rp + i, 8), seg(pp, LANE)] for i in BOTH)
                    g = jnp.concatenate(pair_halves(e, f), axis=0)
                    for part, val in enumerate(split3(g)):
                        t2[seg(12 * h + 3 * t + g3, 16), pl.ds(mult(part * D + n * THIRD + rp * LANE, LANE), LANE)] = val

    def right_half(k):
        n = k // 2
        rows = t2.at[pl.ds(mult((k - 2 * n) * 192, 192), 192)]
        o3[...] = dot6(rows, r3.at[:, pl.ds(mult(n * THIRD, THIRD), THIRD)], D)

    def send_out(m, k):
        @pl.when(m > 0)
        def _():
            wait_bytes(parts(k, 14), rs_send.at[k])

        for j in QUAD:
            y = [o3[seg(t, HALF), seg(j, LANE)] for t in QUAD]
            for sp in BOTH:
                for i, val in enumerate(pair_halves(y[2 * sp], y[2 * sp + 1])):
                    sz[k, j, i, :, seg(sp, LANE)] = val[:PART]
                    sy[k, i, j, :, seg(sp, LANE)] = val[PART:]
        rs_start(lax.rem(m, 2), k)

    def rg_start(c):
        up, low = rbuf.at[c, core, mem, top(HALF)], rbuf.at[c, core, mem, pl.ds(HALF, HALF)]
        for peer in x_peers:
            remote(low, low, rr_send.at[c], rr_first.at[c], peer)
        remote(up, up, rr_send.at[c], rr_first.at[c], ya_peer)
        for peer in x_peers:
            remote(up, up, rr_send.at[c], rr_last.at[c], peer)

    def rg_bytes(n):
        return rbuf.at[0, 0, top(n)]

    def rg_second(c):
        wait_bytes(rg_bytes(2), rr_first.at[c])
        low = rbuf.at[c, core, pl.ds(ya * 4, 4), pl.ds(HALF, HALF)]
        remote(low, low, rr_send.at[c], rr_last.at[c], ya_peer)
        up = rbuf.at[c, core, (1 - ya) * 4 + x, top(HALF)]
        for peer in x_peers:
            remote(up, up, rr_send.at[c], rr_last.at[c], peer)

    def rg_split(c, half):
        def piece(i):
            mp = i // 4
            rr = i - 4 * mp
            for g in TRIO:
                bg = 3 * mp + g
                n = bg // 4
                dst = mult(n * THIRD + (half * 4 + rr) * 64 + (bg - 4 * n) * 16, 16)
                eights = []
                for e in BOTH:
                    hop, off = divmod(2 * g + e, 3)
                    eights.append(rbuf[c, half, 2 * mp + hop, pl.ds(mult(rr * PART + off * 8, 8), 8), :])
                for part, val in enumerate(reversed(split3(jnp.concatenate(eights, axis=0)))):
                    r3[pl.ds(part * D + dst, 16), pl.ds(mult(c * THIRD, THIRD), THIRD)] = val

        loop(16, piece)

    def rg_finish(c):
        wait_bytes(rg_bytes(5), rr_last.at[c])
        part = rbuf.at[c, core]
        remote(part, part, rf_send.at[c], rf_recv.at[c], partner)
        rg_split(c, core)
        wait_bytes(part, rf_recv.at[c])
        rg_split(c, 1 - core)

    for d, peer in enumerate(a_peers[:7]):
        to = lax.rem(row + (d + 1) // 4, 2) * 4 + lax.rem(x + (d + 1) % 4, 4)
        remote(psi_ref.at[to], pbuf.at[mem], ps_send, ps_recv, peer)
    pbuf[mem] = psi_ref[ia8]

    def rt_copy(i):
        return pltpu.make_async_copy(rt_ref.at[pl.ds(mult(core * 96 + i * HALF, 8), HALF)], stage.at[i], st_sem.at[i])

    def el_copy(i, slot):
        h = i // 8
        start = (h * 384 + ia8 * HALF) * 8 + (i - 8 * h) * HALF
        return pltpu.make_async_copy(el_ref.at[pl.ds(mult(start, HALF), HALF)], stage.at[slot], st_sem.at[slot])

    for i in BOTH:
        rt_copy(i).start()

    def init(k):
        for i in range(STEPS):
            xs[i + 1, k] = jnp.zeros((HALF, WIDE), F32)
            vs[i, k] = jnp.zeros((HALF, WIDE), F32)

    loop(NCH, init)
    for ref in (dots, gram, gam, ab_out):
        ref[...] = jnp.zeros_like(ref)

    i0 = lax.broadcasted_iota(jnp.int32, (WIDE, WIDE), 0)
    i1 = lax.broadcasted_iota(jnp.int32, (WIDE, WIDE), 1)
    same = (i0 & 7) == ((i1 >> 3) & 7)
    left = ((i0 >> 3) == i1)[:, :32].astype(BF16)
    right = (((i1 >> 6) * 8 + (i1 & 7)) == i0)[:32].astype(BF16)
    for part, val in enumerate(split3(wsm_ref[...])):
        full = dot(dot(left, val).astype(BF16), right)
        w3[:, seg(part, WIDE)] = jnp.where(same, full, 0.0).astype(BF16)

    wait_bytes(pbuf.at[top(7)], ps_recv)
    for i in range(8):
        for s in QUAD:
            t1[seg(8 * s + i, PART), :LANE] = pbuf[i, seg(s, PART), :]
    for n in TRIO:
        for sp in BOTH:
            tile = jnp.concatenate([t1[seg(6 * sp + 3 * i + n, 64), :LANE] for i in BOTH], axis=0).T
            for h in BOTH:
                xs[0, 2 * n + h, :, seg(sp, LANE)] = tile[seg(h, HALF), :]
        for h in BOTH:
            publish(0, 2 * n + h, True)

    def first_dots(k):
        local_dots(0, k, xs[0, k])

    loop(NCH, first_dots)
    for i in BOTH:
        rt_copy(i).wait()
        for j in QUAD:
            a, b, c = (stage[i, :, seg(3 * j + e, LANE)] for e in TRIO)
            lo = low_half(a.shape)
            for e, val in enumerate((jnp.where(lo, a, b), swap(jnp.where(lo, c, a)), jnp.where(lo, b, c))):
                rbuf[e, core, mem, seg(i, HALF), seg(j, LANE)] = val
    el_copy(0, 0).start()

    def el_piece(i):
        slot = lax.rem(i, 2)

        @pl.when(i < 15)
        def _():
            el_copy(i + 1, 1 - slot).start()

        el_copy(i, slot).wait()
        for c in BOTH:
            for h in BOTH:
                for part, val in enumerate(split3(stage[slot, :, seg(2 * c + h, 384)])):
                    l3[pl.ds(mult(i * HALF, 16), HALF), seg(6 * h + 2 * part + c, 384)] = val

    loop(16, el_piece)
    for k in TRIO:
        ag_second(0, k)
    ag_forward(0, 0, 0)

    def step(m):
        par = lax.rem(m, 2)
        nxt = 1 - par
        more, first, later = m < LAST, m == 0, m > 0

        def finish(k):
            combine(m, k)
            publish(m, k, False)

        def halves(k):
            @pl.when(k == 1)
            def _():
                pl.when(later)(lambda: finish(4))
                ag_forward(par, 1, m)
                ag_second(par, 3)
                pl.when(later)(lambda: finish(5))
                red1_start()

                @pl.when(first)
                def _():
                    ag_second(par, 4)
                    ag_second(par, 5)
                    rg_start(0)

            @pl.when(k == 2)
            def _():
                ag_forward(par, 2, m)
                pl.when(later)(lambda: ag_second(par, 4))
                ag_forward(par, 3, m)
                red_mid(0)
                pl.when(first)(lambda: rg_start(1))

            @pl.when(k == 3)
            def _():
                pl.when(later)(lambda: ag_second(par, 5))

            @pl.when(k == 4)
            def _():
                ag_forward(par, 4, m)
                red1_end(m)
                ag_forward(par, 5, m)

                @pl.when(first)
                def _():
                    rg_second(0)
                    rg_start(2)

            left_half(par, k)

            @pl.when(k == 5)
            def _():
                red_mid(1)
                pl.when(first)(lambda: rg_second(1))

            pl.when(lax.rem(k, 2) == 1)(lambda: mix_chunk(k // 2))

        loop(NCH, halves)
        pl.when(first)(lambda: rg_second(2))

        def advance(k):
            combine(m + 1, k)
            pl.when(more)(lambda: publish(m + 1, k, False))

        def spread(k):
            pl.when(more)(lambda: ag_second(nxt, k))

        def outs(k):
            @pl.when(first & (lax.rem(k, 2) == 0))
            def _():
                rg_finish(k // 2)

            right_half(k)

            @pl.when(k == 3)
            def _():
                rs_second(par, 1)
                red2_end(m, False)

            @pl.when(k == 4)
            def _():
                advance(0)
                rs_second(par, 2)

            @pl.when(k == 5)
            def _():
                rs_second(par, 3)
                spread(0)

            send_out(m, k)

            pl.when(k == 2)(lambda: rs_second(par, 0))
            pl.when(k == 4)(lambda: advance(1))

        loop(NCH, outs)
        advance(2)
        spread(1)
        rs_second(par, 4)
        pl.when(more)(lambda: ag_forward(nxt, 0, 1))
        advance(3)
        rs_second(par, 5)
        spread(2)

    loop(STEPS, step)

    combine(STEPS, 4)
    combine(STEPS, 5)
    red1_start()
    red_mid(0)
    red1_end(STEPS)
    red_mid(1)
    red2_end(STEPS, True)
    for n in TRIO:
        for sp in BOTH:
            rows = [u1[2 * n + h, :, seg(sp, LANE)] for h in BOTH] + [jnp.zeros((32, LANE), F32)]
            tile = jnp.concatenate(rows, axis=0).T
            for s in BOTH:
                for g in range(8):
                    to, off = divmod(8 * n + g, 3)
                    obuf[to, seg(6 * sp + 3 * s + off, 8), :] = tile[seg(8 * s + g, 8), :]
    for d, peer in enumerate(a_peers[:7]):
        to_row = lax.rem(row + (d + 1) // 4, 2)
        to = lax.rem(to_row + yb, 2) * 4 + lax.rem(x + (d + 1) % 4, 4)
        remote(obuf.at[to], obr.at[ia8], ou_send, ou_recv, peer)
    obr[ia8] = obuf[mem]
    for k in range(NCH):
        wait_bytes(parts(k, 14), ag_send.at[k])
        wait_bytes(parts(k, 14), rs_send.at[k])
        wait_bytes(gb.at[0, k, top(8)], fw_send.at[k])
    for c in TRIO:
        wait_bytes(rg_bytes(7), rr_send.at[c])
        wait_bytes(rbuf.at[0, 0], rf_send.at[c])
    wait_bytes(pbuf.at[top(7)], ps_send)
    wait_bytes(obr.at[top(7)], ou_recv)
    wait_bytes(obr.at[top(7)], ou_send)
    v_out[...] = obr[...]


def run_kernel(psi, wsm, el, rt):
    vmem = pl.BlockSpec(memory_space=pltpu.VMEM)
    hbm = pl.BlockSpec(memory_space=pl.ANY)
    dma = pltpu.SemaphoreType.DMA
    six, pair, three = dma((NCH,)), dma((2,)), dma((3,))
    both = dma((2, NCH))
    block = (HALF, WIDE)
    small = pltpu.VMEM((8, 96, LANE), F32)
    return pl.pallas_call(
        kernel,
        out_shape=(jax.ShapeDtypeStruct((8, 96, LANE), F32), jax.ShapeDtypeStruct((8, LANE), F32)),
        in_specs=[vmem, vmem, hbm, hbm],
        out_specs=(vmem, vmem),
        scratch_shapes=[
            pltpu.VMEM((MROWS, 3 * D), BF16),
            pltpu.VMEM((3 * D, D), BF16),
            pltpu.VMEM((WIDE, MROWS), BF16),
            pltpu.VMEM((2, NCH, 16, *block), F32),
            pltpu.VMEM((3 * D, WIDE), BF16),
            pltpu.VMEM((MROWS, WIDE), F32),
            pltpu.VMEM((MROWS, MROWS), BF16),
            pltpu.VMEM((384, 3 * D), BF16),
            pltpu.VMEM((192, THIRD), F32),
            pltpu.VMEM((NCH, 4, 2, PART, WIDE), F32),
            pltpu.VMEM((NCH, 2, 4, PART, WIDE), F32),
            pltpu.VMEM((2, NCH, 14, PART, WIDE), F32),
            pltpu.VMEM((STEPS + 1, NCH, *block), F32),
            pltpu.VMEM((STEPS, NCH, *block), F32),
            pltpu.VMEM((NCH, *block), F32),
            pltpu.VMEM((2, HALF, D), F32),
            pltpu.VMEM((3, 2, 8, 96, THIRD), F32),
            small,
            small,
            small,
            pltpu.VMEM((2 * STEPS, 8, LANE), F32),
            pltpu.VMEM((2, 16, 16, LANE), F32),
            pltpu.VMEM((2, 8, 16, LANE), F32),
            pltpu.VMEM((8, LANE), F32),
            pltpu.VMEM((8, LANE), F32),
            pltpu.VMEM((STEPS, 8, LANE), F32),
            both, both, six, both, both, six, both, six, pair, pair, pair, pair,
            pair, three, three, three, three, three, dma, dma, dma, dma,
        ],
        compiler_params=pltpu.CompilerParams(collective_id=0, has_side_effects=True, vmem_limit_bytes=67043328),
        name="lanczos",
    )(psi, wsm, el, rt)


def solution(mesh):
    grid = Mesh(mesh.devices.reshape(4, 2, 2, 4, 2), AXES)
    psi_spec = P("core", None, None, ("z", "yb", "ya", "x"))

    def local_fn(psi_loc, env_left, env_right, mpo_pair):
        rt = jnp.transpose(env_right, (1, 0, 2)).reshape(192, D)
        psi = jnp.transpose(psi_loc.reshape(2, 8, HALF, 96), (1, 3, 0, 2)).reshape(8, 96, 96)
        psi = jnp.pad(psi, ((0, 0), (0, 0), (0, LANE - 96)))
        wsm = jnp.transpose(mpo_pair.reshape(8, 8, 4, 4), (3, 1, 2, 0)).reshape(32, 32)
        vec, ab = run_kernel(psi, wsm, env_left.reshape(6144, D), rt)
        out = jnp.transpose(vec[:, :, :96].reshape(8, 96, 2, HALF), (2, 0, 3, 1)).reshape(psi_loc.shape)
        return ab[0, :STEPS], ab[1, :STEPS], out

    return jax.shard_map(
        local_fn,
        mesh=grid,
        in_specs=(psi_spec, P("core", None, None), P(("z", "yb", "ya", "x"), None, None), P()),
        out_specs=(P(), P(), psi_spec),
        check_vma=False,
    )
```

time: 393 us -> 341 us (0.87)
  Pallas kernels: 377 us -> 330 us
  local copies, waits for them, and re-layouts: 13.9 us -> 9.84 us
    pallas_call x1, Pallas kernels: 377 us -> 330 us  [run_kernel(): pl.pallas_call(kernel, out_shape=(jax.ShapeDtypeStruct((8, 96, LANE), F32...]
where the time goes in v4:
time: 341 us
  Pallas kernels  330 us (97%)
  local copies, waits for them, and re-layouts  9.84 us (3%)
    pallas_call x1, Pallas kernels, run_kernel(): pl.pallas_call(kernel, out_shape=(jax.ShapeDtypeStruct((8, 96, LANE), F32...  330 us

profile of v4, /device:TPU:1, one launch (start us, length us, event | category | flops | bytes accessed | tf_op | source)
XLA Modules:
  0.0 340.6 jit_solution(18383936902051766522)
XLA Ops:
  0.6 0.9 copy.13
  1.6 0.7 reshape.33.wsm_ref
  2.3 1.4 reshape.30
  3.6 0.0 copy-start
  3.6 0.3 copy.11
  4.0 0.2 copy.12
  4.2 0.8 pad.4.psi_ref
  5.0 0.0 copy-done
  5.0 1.7 copy.14
  6.7 330.0 %lanczos.1 = (f32[8,96,128]{2,1,0:T(8,128)}, f32[8,128]{1,0:T(8,128)}) custom-call(f32[8,96,128]{2,1,0:T(8,128)} %pad.4.psi_ref, f32[32,32]{1,0:T(8,128)} %reshape.33.wsm_ref, f32[6144,1536]{1,0:T(8,128)} %bitcast.23, f32[192,1536]{1,0:T(8,128)} %bitcast.24), custom_call_target="tpu_custom_call" | custom-call | tf_op jit(solution)/shard_map/lanczos/pallas_call | solution.py:595
  336.7 1.3 slice_bitcast_fusion
  338.0 1.2 copy.15
  339.1 0.4 copy.16
  339.5 1.0 reshape.37
Async XLA Ops:
  3.6 1.3 copy-start

commit v5 on v4

--- a/solution.py
+++ b/solution.py
@@ -92,7 +92,7 @@
     psi_ref, wsm_ref, el_ref, rt_ref, v_out, ab_out,
     l3, r3, w3, gb, v3, t1, tq, t2, o3, sz, sy, rsb, xs, vs, u1, stage, rbuf, pbuf, obuf, obr, dots, ra, rb, cg, gam, gram,
     rs_first, rs_last, rs_send, ag_first, ag_last, ag_send, fw_recv, fw_send, ra_recv, ra_send, rb_recv, rb_send,
-    st_sem, rr_first, rr_last, rr_send, rf_recv, rf_send, ps_recv, ps_send, ou_recv, ou_send,
+    st_sem, el_sem, rr_first, rr_last, rr_send, rf_recv, rf_send, ps_recv, ps_send, ou_recv, ou_send,
 ):
     z, yb, ya, x, core = (lax.axis_index(name) for name in AXES)
     row = lax.rem(ya + yb, 2)
@@ -115,10 +115,42 @@
     x_peers, ya_peer = a_peers[:3], a_peers[3]
     z_peers, yb_peer = b_peers[:3], b_peers[3]
 
+    def rt_copy(i):
+        return pltpu.make_async_copy(rt_ref.at[pl.ds(mult(core * 96 + i * HALF, 8), HALF)], stage.at[i], st_sem.at[i])
+
+    psi_copy = pltpu.make_async_copy(psi_ref, obr, ou_recv)
+    psi_copy.start()
+    for i in BOTH:
+        rt_copy(i).start()
+    for c in range(NCH):
+        for h in BOTH:
+            src = el_ref.at[pl.ds(h * 64 + ia8 * 8, 8), :, seg(c, WIDE)]
+            pltpu.make_async_copy(src, gb.at[1, c, pl.ds(8 * h, 8)], el_sem.at[c]).start()
+
     barrier = pltpu.get_barrier_semaphore()
     for peer in a_peers + b_peers:
         pl.semaphore_signal(barrier, inc=1, device_id=peer, device_id_type=MESH)
+
+    def init(k):
+        for i in range(STEPS):
+            xs[i + 1, k] = jnp.zeros((HALF, WIDE), F32)
+            vs[i, k] = jnp.zeros((HALF, WIDE), F32)
+
+    loop(NCH, init)
+    for ref in (dots, gram, gam, ab_out):
+        ref[...] = jnp.zeros_like(ref)
+
+    i0 = lax.broadcasted_iota(jnp.int32, (WIDE, WIDE), 0)
+    i1 = lax.broadcasted_iota(jnp.int32, (WIDE, WIDE), 1)
+    same = (i0 & 7) == ((i1 >> 3) & 7)
+    left = ((i0 >> 3) == i1)[:, :32].astype(BF16)
+    right = (((i1 >> 6) * 8 + (i1 & 7)) == i0)[:32].astype(BF16)
+    for part, val in enumerate(split3(wsm_ref[...])):
+        full = dot(dot(left, val).astype(BF16), right)
+        w3[:, seg(part, WIDE)] = jnp.where(same, full, 0.0).astype(BF16)
+
     pl.semaphore_wait(barrier, len(a_peers) + len(b_peers))
+    psi_copy.wait()
 
     def remote(src, dst, send, recv, peer):
         pltpu.make_async_remote_copy(src_ref=src, dst_ref=dst, send_sem=send, recv_sem=recv, device_id=peer, device_id_type=MESH).start()
@@ -362,49 +394,31 @@
 
         loop(16, piece)
 
-    def rg_finish(c):
+    def rg_forward(c):
         wait_bytes(rg_bytes(5), rr_last.at[c])
         part = rbuf.at[c, core]
         remote(part, part, rf_send.at[c], rf_recv.at[c], partner)
-        rg_split(c, core)
-        wait_bytes(part, rf_recv.at[c])
+
+    def rg_other(c):
+        wait_bytes(rbuf.at[c, 1 - core], rf_recv.at[c])
         rg_split(c, 1 - core)
 
     for d, peer in enumerate(a_peers[:7]):
         to = lax.rem(row + (d + 1) // 4, 2) * 4 + lax.rem(x + (d + 1) % 4, 4)
-        remote(psi_ref.at[to], pbuf.at[mem], ps_send, ps_recv, peer)
-    pbuf[mem] = psi_ref[ia8]
-
-    def rt_copy(i):
-        return pltpu.make_async_copy(rt_ref.at[pl.ds(mult(core * 96 + i * HALF, 8), HALF)], stage.at[i], st_sem.at[i])
-
-    def el_copy(i, slot):
-        h = i // 8
-        start = (h * 384 + ia8 * HALF) * 8 + (i - 8 * h) * HALF
-        return pltpu.make_async_copy(el_ref.at[pl.ds(mult(start, HALF), HALF)], stage.at[slot], st_sem.at[slot])
+        remote(obr.at[to], pbuf.at[mem], ps_send, ps_recv, peer)
+    pbuf[mem] = obr[ia8]
 
     for i in BOTH:
-        rt_copy(i).start()
-
-    def init(k):
-        for i in range(STEPS):
-            xs[i + 1, k] = jnp.zeros((HALF, WIDE), F32)
-            vs[i, k] = jnp.zeros((HALF, WIDE), F32)
-
-    loop(NCH, init)
-    for ref in (dots, gram, gam, ab_out):
-        ref[...] = jnp.zeros_like(ref)
-
-    i0 = lax.broadcasted_iota(jnp.int32, (WIDE, WIDE), 0)
-    i1 = lax.broadcasted_iota(jnp.int32, (WIDE, WIDE), 1)
-    same = (i0 & 7) == ((i1 >> 3) & 7)
-    left = ((i0 >> 3) == i1)[:, :32].astype(BF16)
-    right = (((i1 >> 6) * 8 + (i1 & 7)) == i0)[:32].astype(BF16)
-    for part, val in enumerate(split3(wsm_ref[...])):
-        full = dot(dot(left, val).astype(BF16), right)
-        w3[:, seg(part, WIDE)] = jnp.where(same, full, 0.0).astype(BF16)
+        rt_copy(i).wait()
+        for j in QUAD:
+            a, b, c = (stage[i, :, seg(3 * j + e, LANE)] for e in TRIO)
+            lo = low_half(a.shape)
+            for e, val in enumerate((jnp.where(lo, a, b), swap(jnp.where(lo, c, a)), jnp.where(lo, b, c))):
+                rbuf[e, core, mem, seg(i, HALF), seg(j, LANE)] = val
+    rg_start(0)
 
     wait_bytes(pbuf.at[top(7)], ps_recv)
+    wait_bytes(pbuf.at[top(7)], ps_send)
     for i in range(8):
         for s in QUAD:
             t1[seg(8 * s + i, PART), :LANE] = pbuf[i, seg(s, PART), :]
@@ -413,38 +427,52 @@
             tile = jnp.concatenate([t1[seg(6 * sp + 3 * i + n, 64), :LANE] for i in BOTH], axis=0).T
             for h in BOTH:
                 xs[0, 2 * n + h, :, seg(sp, LANE)] = tile[seg(h, HALF), :]
-        for h in BOTH:
-            publish(0, 2 * n + h, True)
 
     def first_dots(k):
         local_dots(0, k, xs[0, k])
 
-    loop(NCH, first_dots)
-    for i in BOTH:
-        rt_copy(i).wait()
-        for j in QUAD:
-            a, b, c = (stage[i, :, seg(3 * j + e, LANE)] for e in TRIO)
-            lo = low_half(a.shape)
-            for e, val in enumerate((jnp.where(lo, a, b), swap(jnp.where(lo, c, a)), jnp.where(lo, b, c))):
-                rbuf[e, core, mem, seg(i, HALF), seg(j, LANE)] = val
-    el_copy(0, 0).start()
-
     def el_piece(i):
-        slot = lax.rem(i, 2)
-
-        @pl.when(i < 15)
+        for t in range(12):
+            c, h = divmod(t // 3, 2)
+            for part, val in enumerate(split3(gb[1, t // 2, i, :, seg(t % 2, LANE)])):
+                l3[pl.ds(mult(i * HALF, 16), HALF), seg(3 * (6 * h + 2 * part + c) + t % 3, LANE)] = val
+
+    for c in range(NCH):
+        wait_bytes(gb.at[1, c], el_sem.at[c])
+
+    def lead(e):
+        @pl.when(e == 0)
         def _():
-            el_copy(i + 1, 1 - slot).start()
-
-        el_copy(i, slot).wait()
-        for c in BOTH:
-            for h in BOTH:
-                for part, val in enumerate(split3(stage[slot, :, seg(2 * c + h, 384)])):
-                    l3[pl.ds(mult(i * HALF, 16), HALF), seg(6 * h + 2 * part + c, 384)] = val
-
-    loop(16, el_piece)
-    for k in TRIO:
-        ag_second(0, k)
+            for k in TRIO:
+                publish(0, k, True)
+
+        @pl.when(e == 1)
+        def _():
+            publish(0, 3, True)
+            publish(0, 4, True)
+            loop(NCH, first_dots)
+
+        @pl.when(e == 2)
+        def _():
+            ag_second(0, 0)
+            rg_second(0)
+            ag_second(0, 1)
+            publish(0, 5, True)
+
+        @pl.when(e == 3)
+        def _():
+            ag_second(0, 3)
+            ag_second(0, 2)
+            rg_forward(0)
+
+        loop(4, lambda i: el_piece(4 * e + i))
+
+    loop(4, lead)
+    ag_second(0, 5)
+    rg_start(1)
+    rg_split(0, core)
+    rg_other(0)
+    ag_second(0, 4)
     ag_forward(0, 0, 0)
 
     def step(m):
@@ -459,52 +487,41 @@
         def halves(k):
             @pl.when(k == 1)
             def _():
-                pl.when(later)(lambda: finish(4))
                 ag_forward(par, 1, m)
-                ag_second(par, 3)
-                pl.when(later)(lambda: finish(5))
+
+                @pl.when(later)
+                def _():
+                    ag_second(par, 3)
+                    finish(5)
+
                 red1_start()
 
                 @pl.when(first)
                 def _():
-                    ag_second(par, 4)
-                    ag_second(par, 5)
-                    rg_start(0)
+                    rg_start(2)
+                    rg_second(1)
 
             @pl.when(k == 2)
             def _():
-                ag_forward(par, 2, m)
                 pl.when(later)(lambda: ag_second(par, 4))
                 ag_forward(par, 3, m)
                 red_mid(0)
-                pl.when(first)(lambda: rg_start(1))
-
-            @pl.when(k == 3)
-            def _():
                 pl.when(later)(lambda: ag_second(par, 5))
 
             @pl.when(k == 4)
             def _():
-                ag_forward(par, 4, m)
                 red1_end(m)
                 ag_forward(par, 5, m)
-
-                @pl.when(first)
-                def _():
-                    rg_second(0)
-                    rg_start(2)
+                pl.when(first)(lambda: rg_second(2))
 
             left_half(par, k)
 
-            @pl.when(k == 5)
-            def _():
-                red_mid(1)
-                pl.when(first)(lambda: rg_second(1))
-
+            pl.when(k == 1)(lambda: ag_forward(par, 2, m))
+            pl.when(k == 3)(lambda: ag_forward(par, 4, m))
             pl.when(lax.rem(k, 2) == 1)(lambda: mix_chunk(k // 2))
 
         loop(NCH, halves)
-        pl.when(first)(lambda: rg_second(2))
+        red_mid(1)
 
         def advance(k):
             combine(m + 1, k)
@@ -514,44 +531,49 @@
             pl.when(more)(lambda: ag_second(nxt, k))
 
         def outs(k):
-            @pl.when(first & (lax.rem(k, 2) == 0))
+            pl.when(first & (k == 1))(lambda: rg_forward(1))
+
+            @pl.when(first & (k == 2))
             def _():
-                rg_finish(k // 2)
-
+                rg_split(1, core)
+                rg_other(1)
+                rg_forward(2)
+                rg_split(2, core)
+
+            pl.when(first & (k == 4))(lambda: rg_other(2))
             right_half(k)
-
-            @pl.when(k == 3)
+            pl.when(k == 3)(lambda: rs_second(par, 1))
+
+            @pl.when(k == 5)
             def _():
-                rs_second(par, 1)
+                advance(1)
+                rs_second(par, 3)
+
+            send_out(m, k)
+
+            @pl.when(k == 2)
+            def _():
                 red2_end(m, False)
+                rs_second(par, 0)
 
             @pl.when(k == 4)
             def _():
+                rs_second(par, 2)
                 advance(0)
-                rs_second(par, 2)
-
-            @pl.when(k == 5)
-            def _():
-                rs_second(par, 3)
-                spread(0)
-
-            send_out(m, k)
-
-            pl.when(k == 2)(lambda: rs_second(par, 0))
-            pl.when(k == 4)(lambda: advance(1))
 
         loop(NCH, outs)
+        spread(0)
+        rs_second(par, 4)
         advance(2)
         spread(1)
-        rs_second(par, 4)
+        advance(3)
         pl.when(more)(lambda: ag_forward(nxt, 0, 1))
-        advance(3)
         rs_second(par, 5)
         spread(2)
+        advance(4)
 
     loop(STEPS, step)
 
-    combine(STEPS, 4)
     combine(STEPS, 5)
     red1_start()
     red_mid(0)
@@ -578,7 +600,6 @@
     for c in TRIO:
         wait_bytes(rg_bytes(7), rr_send.at[c])
         wait_bytes(rbuf.at[0, 0], rf_send.at[c])
-    wait_bytes(pbuf.at[top(7)], ps_send)
     wait_bytes(obr.at[top(7)], ou_recv)
     wait_bytes(obr.at[top(7)], ou_send)
     v_out[...] = obr[...]
@@ -595,7 +616,7 @@
     return pl.pallas_call(
         kernel,
         out_shape=(jax.ShapeDtypeStruct((8, 96, LANE), F32), jax.ShapeDtypeStruct((8, LANE), F32)),
-        in_specs=[vmem, vmem, hbm, hbm],
+        in_specs=[hbm, vmem, hbm, hbm],
         out_specs=(vmem, vmem),
         scratch_shapes=[
             pltpu.VMEM((MROWS, 3 * D), BF16),
@@ -625,7 +646,7 @@
             pltpu.VMEM((8, LANE), F32),
             pltpu.VMEM((STEPS, 8, LANE), F32),
             both, both, six, both, both, six, both, six, pair, pair, pair, pair,
-            pair, three, three, three, three, three, dma, dma, dma, dma,
+            pair, six, three, three, three, three, three, dma, dma, dma, dma,
         ],
         compiler_params=pltpu.CompilerParams(collective_id=0, has_side_effects=True, vmem_limit_bytes=67043328),
         name="lanczos",
@@ -641,7 +662,7 @@
         psi = jnp.transpose(psi_loc.reshape(2, 8, HALF, 96), (1, 3, 0, 2)).reshape(8, 96, 96)
         psi = jnp.pad(psi, ((0, 0), (0, 0), (0, LANE - 96)))
         wsm = jnp.transpose(mpo_pair.reshape(8, 8, 4, 4), (3, 1, 2, 0)).reshape(32, 32)
-        vec, ab = run_kernel(psi, wsm, env_left.reshape(6144, D), rt)
+        vec, ab = run_kernel(psi, wsm, env_left.reshape(LANE, HALF, D), rt)
         out = jnp.transpose(vec[:, :, :96].reshape(8, 96, 2, HALF), (2, 0, 3, 1)).reshape(psi_loc.shape)
         return ab[0, :STEPS], ab[1, :STEPS], out
 

time: 341 us -> 330 us (0.968)
  Pallas kernels: 330 us -> 319 us
    pallas_call x1, Pallas kernels: 330 us -> 319 us  [run_kernel(): pl.pallas_call(kernel, out_shape=(jax.ShapeDtypeStruct((8, 96, LANE), F32...]
where the time goes in v5:
time: 330 us; the launch traced here: 329 us
  Pallas kernels  319 us (97%)
  local copies, waits for them, and re-layouts  9.84 us (3%)
    pallas_call x1, Pallas kernels, run_kernel(): pl.pallas_call(kernel, out_shape=(jax.ShapeDtypeStruct((8, 96, LANE), F32...  319 us

profile of v5, /device:TPU:1, one launch (start us, length us, event | category | flops | bytes accessed | tf_op | source)
XLA Modules:
  0.0 329.4 jit_solution(11487427717728538469)
XLA Ops:
  0.6 0.9 copy.13
  1.6 0.7 reshape.33.wsm_ref
  2.3 1.4 reshape.30
  3.6 0.0 copy-start
  3.6 0.3 copy.11
  4.0 0.2 copy.12
  4.2 0.8 pad.4.psi_ref
  5.0 0.0 copy-done
  5.0 1.7 copy.14
  6.7 318.8 %lanczos.1 = (f32[8,96,128]{2,1,0:T(8,128)}, f32[8,128]{1,0:T(8,128)}) custom-call(f32[8,96,128]{2,1,0:T(8,128)} %pad.4.psi_ref, f32[32,32]{1,0:T(8,128)} %reshape.33.wsm_ref, f32[128,48,1536]{2,1,0:T(8,128)} %bitcast.23, f32[192,1536]{1,0:T(8,128)} %bitcast.24), custom_call_target="tpu_custom_call" | custom-call | tf_op jit(solution)/shard_map/lanczos/pallas_call | solution.py:616
  325.5 1.3 slice_bitcast_fusion
  326.8 1.2 copy.15
  327.9 0.4 copy.16
  328.3 1.0 reshape.37
Async XLA Ops:
  3.6 1.3 copy-start

commit v6 on v5

--- a/solution.py
+++ b/solution.py
@@ -92,7 +92,7 @@
     psi_ref, wsm_ref, el_ref, rt_ref, v_out, ab_out,
     l3, r3, w3, gb, v3, t1, tq, t2, o3, sz, sy, rsb, xs, vs, u1, stage, rbuf, pbuf, obuf, obr, dots, ra, rb, cg, gam, gram,
     rs_first, rs_last, rs_send, ag_first, ag_last, ag_send, fw_recv, fw_send, ra_recv, ra_send, rb_recv, rb_send,
-    st_sem, el_sem, rr_first, rr_last, rr_send, rf_recv, rf_send, ps_recv, ps_send, ou_recv, ou_send,
+    st_sem, el_sem, rr_first, rr_last, rr_send, rf_recv, rf_send, ps_recv, ps_send, in_sem, ex_send, ex_recv,
 ):
     z, yb, ya, x, core = (lax.axis_index(name) for name in AXES)
     row = lax.rem(ya + yb, 2)
@@ -115,13 +115,14 @@
     x_peers, ya_peer = a_peers[:3], a_peers[3]
     z_peers, yb_peer = b_peers[:3], b_peers[3]
 
-    def rt_copy(i):
-        return pltpu.make_async_copy(rt_ref.at[pl.ds(mult(core * 96 + i * HALF, 8), HALF)], stage.at[i], st_sem.at[i])
-
-    psi_copy = pltpu.make_async_copy(psi_ref, obr, ou_recv)
+    def rt_copy(p):
+        dst = stage.at[p // 2, pl.ds(PART * (p % 2), PART)]
+        return pltpu.make_async_copy(rt_ref.at[:, core * 4 + p, :], dst, st_sem.at[p])
+
+    psi_copy = pltpu.make_async_copy(psi_ref, obr, in_sem)
     psi_copy.start()
-    for i in BOTH:
-        rt_copy(i).start()
+    for p in QUAD:
+        rt_copy(p).start()
     for c in range(NCH):
         for h in BOTH:
             src = el_ref.at[pl.ds(h * 64 + ia8 * 8, 8), :, seg(c, WIDE)]
@@ -281,6 +282,29 @@
 
         loop(NCH, piece)
         red_rows(1, [(i, i) for i in range(STEPS)] + [(STEPS, 8)])
+
+    def spare(i, slot):
+        return rbuf.at[i // 2, lax.rem(i, 2), slot, :, top(LANE)]
+
+    def export_pack(vec):
+        for n in TRIO:
+            for sp in BOTH:
+                rows = [vec[2 * n + h, :, seg(sp, LANE)] for h in BOTH] + [jnp.zeros((32, LANE), F32)]
+                tile = jnp.concatenate(rows, axis=0).T
+                for s in BOTH:
+                    for g in range(8):
+                        to, off = divmod(8 * n + g, 3)
+                        obuf[to, seg(6 * sp + 3 * s + off, 8), :] = tile[seg(8 * s + g, 8), :]
+
+    def export_send(i):
+        for d, peer in enumerate(a_peers[:7]):
+            to_row = lax.rem(row + (d + 1) // 4, 2)
+            to = lax.rem(to_row + yb, 2) * 4 + lax.rem(x + (d + 1) % 4, 4)
+            remote(obuf.at[to], spare(i, ia8), ex_send, ex_recv.at[i], peer)
+        spare(i, ia8)[...] = obuf[mem]
+
+    def export_done():
+        wait_bytes(obuf.at[top(7)], ex_send)
 
     def red2_end(m, last):
         total = red_end(1)
@@ -295,18 +319,27 @@
         record(1, m, beta)
         gam[...] = cg[...] + d8
         gam[row1(STEPS), :] = inv
-        scale = wide(inv * math.sqrt(float(4 * D * D)) if last else inv)
-
-        def piece(k):
-            cur = u1[k]
-            for i in range(STEPS):
-                cur = cur - wide(d8[row1(i)]) * vs[i, k]
-            if last:
-                u1[k] = cur * scale
-            else:
-                vs[m, k] = cur * scale
-
-        loop(NCH, piece)
+        if last:
+            scale = inv * math.sqrt(float(4 * D * D))
+            for i in range(NCH):
+                wait_bytes(obuf.at[top(7)], ex_recv.at[i])
+
+            def final(j):
+                cur = spare(STEPS, j)[...]
+                for i in range(STEPS):
+                    cur = cur - d8[row1(i)] * spare(i, j)[...]
+                v_out[j] = (cur * scale)[:, :96]
+
+            loop(8, final)
+        else:
+
+            def piece(k):
+                cur = u1[k]
+                for i in range(STEPS):
+                    cur = cur - wide(d8[row1(i)]) * vs[i, k]
+                vs[m, k] = cur * wide(inv)
+
+            loop(NCH, piece)
 
     def left_half(par, k):
         wait_bytes(gb.at[par, k, pl.ds((1 - core) * 8, 8)], fw_recv.at[par, k])
@@ -408,8 +441,9 @@
         remote(obr.at[to], pbuf.at[mem], ps_send, ps_recv, peer)
     pbuf[mem] = obr[ia8]
 
+    for p in QUAD:
+        rt_copy(p).wait()
     for i in BOTH:
-        rt_copy(i).wait()
         for j in QUAD:
             a, b, c = (stage[i, :, seg(3 * j + e, LANE)] for e in TRIO)
             lo = low_half(a.shape)
@@ -421,7 +455,7 @@
     wait_bytes(pbuf.at[top(7)], ps_send)
     for i in range(8):
         for s in QUAD:
-            t1[seg(8 * s + i, PART), :LANE] = pbuf[i, seg(s, PART), :]
+            t1[seg(8 * s + i, PART), :96] = pbuf[i, seg(s, PART), :]
     for n in TRIO:
         for sp in BOTH:
             tile = jnp.concatenate([t1[seg(6 * sp + 3 * i + n, 64), :LANE] for i in BOTH], axis=0).T
@@ -521,6 +555,7 @@
             pl.when(lax.rem(k, 2) == 1)(lambda: mix_chunk(k // 2))
 
         loop(NCH, halves)
+        pl.when(later)(lambda: export_send(m - 1))
         red_mid(1)
 
         def advance(k):
@@ -562,6 +597,13 @@
                 advance(0)
 
         loop(NCH, outs)
+
+        @pl.when(first)
+        def _():
+            for c in TRIO:
+                wait_bytes(rg_bytes(7), rr_send.at[c])
+                wait_bytes(rbuf.at[0, 0], rf_send.at[c])
+
         spread(0)
         rs_second(par, 4)
         advance(2)
@@ -571,38 +613,26 @@
         rs_second(par, 5)
         spread(2)
         advance(4)
+        pl.when(later)(export_done)
+        export_pack(vs.at[m])
 
     loop(STEPS, step)
 
+    export_send(LAST)
     combine(STEPS, 5)
     red1_start()
     red_mid(0)
     red1_end(STEPS)
+    export_done()
+    export_pack(u1)
+    export_send(STEPS)
     red_mid(1)
     red2_end(STEPS, True)
-    for n in TRIO:
-        for sp in BOTH:
-            rows = [u1[2 * n + h, :, seg(sp, LANE)] for h in BOTH] + [jnp.zeros((32, LANE), F32)]
-            tile = jnp.concatenate(rows, axis=0).T
-            for s in BOTH:
-                for g in range(8):
-                    to, off = divmod(8 * n + g, 3)
-                    obuf[to, seg(6 * sp + 3 * s + off, 8), :] = tile[seg(8 * s + g, 8), :]
-    for d, peer in enumerate(a_peers[:7]):
-        to_row = lax.rem(row + (d + 1) // 4, 2)
-        to = lax.rem(to_row + yb, 2) * 4 + lax.rem(x + (d + 1) % 4, 4)
-        remote(obuf.at[to], obr.at[ia8], ou_send, ou_recv, peer)
-    obr[ia8] = obuf[mem]
+    export_done()
     for k in range(NCH):
         wait_bytes(parts(k, 14), ag_send.at[k])
         wait_bytes(parts(k, 14), rs_send.at[k])
         wait_bytes(gb.at[0, k, top(8)], fw_send.at[k])
-    for c in TRIO:
-        wait_bytes(rg_bytes(7), rr_send.at[c])
-        wait_bytes(rbuf.at[0, 0], rf_send.at[c])
-    wait_bytes(obr.at[top(7)], ou_recv)
-    wait_bytes(obr.at[top(7)], ou_send)
-    v_out[...] = obr[...]
 
 
 def run_kernel(psi, wsm, el, rt):
@@ -612,10 +642,10 @@
     six, pair, three = dma((NCH,)), dma((2,)), dma((3,))
     both = dma((2, NCH))
     block = (HALF, WIDE)
-    small = pltpu.VMEM((8, 96, LANE), F32)
+    start = pltpu.VMEM((8, 96, 96), F32)
     return pl.pallas_call(
         kernel,
-        out_shape=(jax.ShapeDtypeStruct((8, 96, LANE), F32), jax.ShapeDtypeStruct((8, LANE), F32)),
+        out_shape=(jax.ShapeDtypeStruct((8, 96, 96), F32), jax.ShapeDtypeStruct((8, LANE), F32)),
         in_specs=[hbm, vmem, hbm, hbm],
         out_specs=(vmem, vmem),
         scratch_shapes=[
@@ -636,9 +666,9 @@
             pltpu.VMEM((NCH, *block), F32),
             pltpu.VMEM((2, HALF, D), F32),
             pltpu.VMEM((3, 2, 8, 96, THIRD), F32),
-            small,
-            small,
-            small,
+            start,
+            pltpu.VMEM((8, 96, LANE), F32),
+            start,
             pltpu.VMEM((2 * STEPS, 8, LANE), F32),
             pltpu.VMEM((2, 16, 16, LANE), F32),
             pltpu.VMEM((2, 8, 16, LANE), F32),
@@ -646,7 +676,7 @@
             pltpu.VMEM((8, LANE), F32),
             pltpu.VMEM((STEPS, 8, LANE), F32),
             both, both, six, both, both, six, both, six, pair, pair, pair, pair,
-            pair, six, three, three, three, three, three, dma, dma, dma, dma,
+            dma((4,)), six, three, three, three, three, three, dma, dma, dma, dma, six,
         ],
         compiler_params=pltpu.CompilerParams(collective_id=0, has_side_effects=True, vmem_limit_bytes=67043328),
         name="lanczos",
@@ -658,12 +688,10 @@
     psi_spec = P("core", None, None, ("z", "yb", "ya", "x"))
 
     def local_fn(psi_loc, env_left, env_right, mpo_pair):
-        rt = jnp.transpose(env_right, (1, 0, 2)).reshape(192, D)
         psi = jnp.transpose(psi_loc.reshape(2, 8, HALF, 96), (1, 3, 0, 2)).reshape(8, 96, 96)
-        psi = jnp.pad(psi, ((0, 0), (0, 0), (0, LANE - 96)))
         wsm = jnp.transpose(mpo_pair.reshape(8, 8, 4, 4), (3, 1, 2, 0)).reshape(32, 32)
-        vec, ab = run_kernel(psi, wsm, env_left.reshape(LANE, HALF, D), rt)
-        out = jnp.transpose(vec[:, :, :96].reshape(8, 96, 2, HALF), (2, 0, 3, 1)).reshape(psi_loc.shape)
+        vec, ab = run_kernel(psi, wsm, env_left.reshape(LANE, HALF, D), env_right)
+        out = jnp.transpose(vec.reshape(8, 96, 2, HALF), (2, 0, 3, 1)).reshape(psi_loc.shape)
         return ab[0, :STEPS], ab[1, :STEPS], out
 
     return jax.shard_map(

time: 330 us -> 323 us (0.979)
  Pallas kernels: 319 us -> 314 us
    pallas_call x1, Pallas kernels: 319 us -> 314 us  [run_kernel(): pl.pallas_call(kernel, out_shape=(jax.ShapeDtypeStruct((8, 96, 96), F32),...]
where the time goes in v6:
time: 323 us
  Pallas kernels  314 us (97%)
  local copies, waits for them, and re-layouts  8.09 us (3%)
    pallas_call x1, Pallas kernels, run_kernel(): pl.pallas_call(kernel, out_shape=(jax.ShapeDtypeStruct((8, 96, 96), F32),...  314 us

profile of v6, /device:TPU:1, one launch (start us, length us, event | category | flops | bytes accessed | tf_op | source)
XLA Modules:
  0.0 322.9 jit_solution(6499252262827746374)
XLA Ops:
  0.6 1.4 reshape.27
  2.0 0.3 copy.10
  2.3 0.9 copy.12.psi_ref
  3.3 0.9 copy.11
  4.2 0.7 reshape.30.wsm_ref
  4.9 314.2 %lanczos.1 = (f32[8,96,96]{2,1,0:T(8,128)}, f32[8,128]{1,0:T(8,128)}) custom-call(f32[8,96,96]{2,1,0:T(8,128)} %copy.12.psi_ref, f32[32,32]{1,0:T(8,128)} %reshape.30.wsm_ref, f32[128,48,1536]{2,1,0:T(8,128)} %bitcast.20, f32[24,8,1536]{2,1,0:T(8,128)} %rt_ref.1), custom_call_target="tpu_custom_call" | custom-call | tf_op jit(solution)/shard_map/lanczos/pallas_call | solution.py:646
  319.1 1.3 slice_bitcast_fusion
  320.3 1.2 copy.13
  321.5 0.4 copy.14
  321.9 1.0 reshape.33

commit v7 on v6

--- a/solution.py
+++ b/solution.py
@@ -193,6 +193,16 @@
 
         part = gb.at[par, k, pl.ds(core * 8, 8)]
         remote(part, part, fw_send.at[k], fw_recv.at[par, k], partner)
+        split_blocks(par, k, core)
+
+    def split_blocks(par, k, who):
+        base = 3 * MROWS * lax.rem(k, 2) + who * 384
+
+        def piece(i):
+            for part, val in enumerate(reversed(split3(gb[par, k, who * 8 + i]))):
+                v3[pl.ds(mult(base + part * MROWS + i * HALF, 16), HALF), :] = val
+
+        loop(8, piece)
 
     def rs_start(par, k):
         remote(sy.at[k, 1 - yb], rsb.at[par, k, pl.ds(6, 4)], rs_send.at[k], rs_first.at[par, k], yb_peer)
@@ -343,14 +353,9 @@
 
     def left_half(par, k):
         wait_bytes(gb.at[par, k, pl.ds((1 - core) * 8, 8)], fw_recv.at[par, k])
+        split_blocks(par, k, 1 - core)
         h = lax.rem(k, 2)
         base = mult(3 * MROWS * h, 3 * MROWS)
-
-        def piece(i):
-            for part, val in enumerate(reversed(split3(gb[par, k, i]))):
-                v3[pl.ds(mult(base + part * MROWS + i * HALF, 16), HALF), :] = val
-
-        loop(16, piece)
         val = dot6(l3.at[:, pl.ds(base, 3 * MROWS)], v3.at[pl.ds(base, 3 * MROWS)], MROWS)
         t1[...] = jnp.where(h == 0, 0.0, t1[...]) + val
 
@@ -410,31 +415,31 @@
         for peer in x_peers:
             remote(up, up, rr_send.at[c], rr_last.at[c], peer)
 
-    def rg_split(c, half):
+    def rg_split(c):
         def piece(i):
-            mp = i // 4
-            rr = i - 4 * mp
-            for g in TRIO:
-                bg = 3 * mp + g
-                n = bg // 4
-                dst = mult(n * THIRD + (half * 4 + rr) * 64 + (bg - 4 * n) * 16, 16)
+            turn = i // 4
+            rr = i - 4 * turn
+            half = lax.rem(core + turn, 2)
+
+            @pl.when(i == 4)
+            def _():
+                wait_bytes(rbuf.at[c, half], rf_recv.at[c])
+
+            for bg in range(12):
+                dst = mult((bg // 4) * THIRD + (half * 4 + rr) * 64 + (bg % 4) * 16, 16)
                 eights = []
                 for e in BOTH:
-                    hop, off = divmod(2 * g + e, 3)
-                    eights.append(rbuf[c, half, 2 * mp + hop, pl.ds(mult(rr * PART + off * 8, 8), 8), :])
+                    who, off = divmod(2 * bg + e, 3)
+                    eights.append(rbuf[c, half, who, pl.ds(mult(rr * PART + off * 8, 8), 8), :])
                 for part, val in enumerate(reversed(split3(jnp.concatenate(eights, axis=0)))):
                     r3[pl.ds(part * D + dst, 16), pl.ds(mult(c * THIRD, THIRD), THIRD)] = val
 
-        loop(16, piece)
+        loop(8, piece)
 
     def rg_forward(c):
         wait_bytes(rg_bytes(5), rr_last.at[c])
         part = rbuf.at[c, core]
         remote(part, part, rf_send.at[c], rf_recv.at[c], partner)
-
-    def rg_other(c):
-        wait_bytes(rbuf.at[c, 1 - core], rf_recv.at[c])
-        rg_split(c, 1 - core)
 
     for d, peer in enumerate(a_peers[:7]):
         to = lax.rem(row + (d + 1) // 4, 2) * 4 + lax.rem(x + (d + 1) % 4, 4)
@@ -504,8 +509,7 @@
     loop(4, lead)
     ag_second(0, 5)
     rg_start(1)
-    rg_split(0, core)
-    rg_other(0)
+    rg_split(0)
     ag_second(0, 4)
     ag_forward(0, 0, 0)
 
@@ -570,12 +574,10 @@
 
             @pl.when(first & (k == 2))
             def _():
-                rg_split(1, core)
-                rg_other(1)
+                rg_split(1)
                 rg_forward(2)
-                rg_split(2, core)
-
-            pl.when(first & (k == 4))(lambda: rg_other(2))
+
+            pl.when(first & (k == 4))(lambda: rg_split(2))
             right_half(k)
             pl.when(k == 3)(lambda: rs_second(par, 1))
 

time: 323 us -> 321 us (level)
  no operation moved by 1% of the time
where the time goes in v7:
time: 321 us; the launch traced here: 320 us
  Pallas kernels  312 us (97%)
  local copies, waits for them, and re-layouts  8.09 us (3%)
    pallas_call x1, Pallas kernels, run_kernel(): pl.pallas_call(kernel, out_shape=(jax.ShapeDtypeStruct((8, 96, 96), F32),...  312 us

profile of v7, /device:TPU:1, one launch (start us, length us, event | category | flops | bytes accessed | tf_op | source)
XLA Modules:
  0.0 320.5 jit_solution(2595049154536755873)
XLA Ops:
  0.6 1.4 reshape.27
  2.0 0.3 copy.10
  2.3 0.9 copy.12.psi_ref
  3.3 0.9 copy.11
  4.2 0.7 reshape.30.wsm_ref
  4.9 311.7 %lanczos.1 = (f32[8,96,96]{2,1,0:T(8,128)}, f32[8,128]{1,0:T(8,128)}) custom-call(f32[8,96,96]{2,1,0:T(8,128)} %copy.12.psi_ref, f32[32,32]{1,0:T(8,128)} %reshape.30.wsm_ref, f32[128,48,1536]{2,1,0:T(8,128)} %bitcast.20, f32[24,8,1536]{2,1,0:T(8,128)} %rt_ref.1), custom_call_target="tpu_custom_call" | custom-call | tf_op jit(solution)/shard_map/lanczos/pallas_call | solution.py:648
  316.6 1.3 slice_bitcast_fusion
  317.9 1.2 copy.13
  319.1 0.4 copy.14
  319.5 1.0 reshape.33

commit v8 on v7

--- a/solution.py
+++ b/solution.py
@@ -90,7 +90,7 @@
 
 def kernel(
     psi_ref, wsm_ref, el_ref, rt_ref, v_out, ab_out,
-    l3, r3, w3, gb, v3, t1, tq, t2, o3, sz, sy, rsb, xs, vs, u1, stage, rbuf, pbuf, obuf, obr, dots, ra, rb, cg, gam, gram,
+    l3, r3, w3, gb, v3, t1, tq, t2, o3, sz, sy, rsb, xs, vs, u1, stage, rbuf, pbuf, obuf, obr, pin, dots, ra, rb, cg, gam, gram,
     rs_first, rs_last, rs_send, ag_first, ag_last, ag_send, fw_recv, fw_send, ra_recv, ra_send, rb_recv, rb_send,
     st_sem, el_sem, rr_first, rr_last, rr_send, rf_recv, rf_send, ps_recv, ps_send, in_sem, ex_send, ex_recv,
 ):
@@ -119,7 +119,7 @@
         dst = stage.at[p // 2, pl.ds(PART * (p % 2), PART)]
         return pltpu.make_async_copy(rt_ref.at[:, core * 4 + p, :], dst, st_sem.at[p])
 
-    psi_copy = pltpu.make_async_copy(psi_ref, obr, in_sem)
+    psi_copy = pltpu.make_async_copy(psi_ref, pin, in_sem)
     psi_copy.start()
     for p in QUAD:
         rt_copy(p).start()
@@ -150,8 +150,10 @@
         full = dot(dot(left, val).astype(BF16), right)
         w3[:, seg(part, WIDE)] = jnp.where(same, full, 0.0).astype(BF16)
 
+    psi_copy.wait()
+    for j in range(8):
+        obr[j] = jnp.concatenate([pin[:, seg(8 * h + j, HALF)] for h in BOTH], axis=1)
     pl.semaphore_wait(barrier, len(a_peers) + len(b_peers))
-    psi_copy.wait()
 
     def remote(src, dst, send, recv, peer):
         pltpu.make_async_remote_copy(src_ref=src, dst_ref=dst, send_sem=send, recv_sem=recv, device_id=peer, device_id_type=MESH).start()
@@ -338,9 +340,12 @@
                 cur = spare(STEPS, j)[...]
                 for i in range(STEPS):
                     cur = cur - d8[row1(i)] * spare(i, j)[...]
-                v_out[j] = (cur * scale)[:, :96]
-
+                obuf[j] = cur * scale
+
+            export_done()
             loop(8, final)
+            for h in BOTH:
+                v_out[:, seg(h, 384)] = jnp.concatenate([obuf[j, :, seg(h, HALF)] for j in range(8)], axis=1)
         else:
 
             def piece(k):
@@ -630,7 +635,6 @@
     export_send(STEPS)
     red_mid(1)
     red2_end(STEPS, True)
-    export_done()
     for k in range(NCH):
         wait_bytes(parts(k, 14), ag_send.at[k])
         wait_bytes(parts(k, 14), rs_send.at[k])
@@ -647,7 +651,7 @@
     start = pltpu.VMEM((8, 96, 96), F32)
     return pl.pallas_call(
         kernel,
-        out_shape=(jax.ShapeDtypeStruct((8, 96, 96), F32), jax.ShapeDtypeStruct((8, LANE), F32)),
+        out_shape=(jax.ShapeDtypeStruct((96, MROWS), F32), jax.ShapeDtypeStruct((8, LANE), F32)),
         in_specs=[hbm, vmem, hbm, hbm],
         out_specs=(vmem, vmem),
         scratch_shapes=[
@@ -671,6 +675,7 @@
             start,
             pltpu.VMEM((8, 96, LANE), F32),
             start,
+            pltpu.VMEM((96, MROWS), F32),
             pltpu.VMEM((2 * STEPS, 8, LANE), F32),
             pltpu.VMEM((2, 16, 16, LANE), F32),
             pltpu.VMEM((2, 8, 16, LANE), F32),
@@ -690,10 +695,10 @@
     psi_spec = P("core", None, None, ("z", "yb", "ya", "x"))
 
     def local_fn(psi_loc, env_left, env_right, mpo_pair):
-        psi = jnp.transpose(psi_loc.reshape(2, 8, HALF, 96), (1, 3, 0, 2)).reshape(8, 96, 96)
+        psi = jnp.transpose(psi_loc, (1, 2, 3, 0)).reshape(96, MROWS)
         wsm = jnp.transpose(mpo_pair.reshape(8, 8, 4, 4), (3, 1, 2, 0)).reshape(32, 32)
         vec, ab = run_kernel(psi, wsm, env_left.reshape(LANE, HALF, D), env_right)
-        out = jnp.transpose(vec.reshape(8, 96, 2, HALF), (2, 0, 3, 1)).reshape(psi_loc.shape)
+        out = jnp.transpose(vec.reshape(2, 2, PART, MROWS), (3, 0, 1, 2))
         return ab[0, :STEPS], ab[1, :STEPS], out
 
     return jax.shard_map(

time: 321 us -> 317 us (0.988)
  local copies, waits for them, and re-layouts: 8.09 us -> 4.61 us
    reshape x3 -> x0, local copies, waits for them, and re-layouts: 3.3 us -> none  [the longest x1 1.36 us: local_fn(): psi_loc.reshape(2, 8, HALF, 96)]
where the time goes in v8:
time: 317 us
  Pallas kernels  312 us (98%)
  local copies, waits for them, and re-layouts  4.61 us (1%)
    pallas_call x1, Pallas kernels, run_kernel(): pl.pallas_call(kernel, out_shape=(jax.ShapeDtypeStruct((96, MROWS), F32),...  312 us

profile of v8, /device:TPU:1, one launch (start us, length us, event | category | flops | bytes accessed | tf_op | source)
XLA Modules:
  0.0 317.1 jit_solution(16645030910287518293)
XLA Ops:
  0.6 0.9 copy.7
  1.6 0.7 reshape.23.wsm_ref
  2.3 311.8 %lanczos.1 = (f32[96,768]{1,0:T(8,128)}, f32[8,128]{1,0:T(8,128)}) custom-call(f32[96,768]{1,0:T(8,128)} %bitcast.14, f32[32,32]{1,0:T(8,128)} %reshape.23.wsm_ref, f32[128,48,1536]{2,1,0:T(8,128)} %bitcast.13, f32[24,8,1536]{2,1,0:T(8,128)} %rt_ref.1), custom_call_target="tpu_custom_call" | custom-call | tf_op jit(solution)/shard_map/lanczos/pallas_call | solution.py:652
  314.1 1.3 slice_bitcast_fusion
  315.4 1.7 copy.9

commit v9 on v8

--- a/solution.py
+++ b/solution.py
@@ -92,7 +92,7 @@
     psi_ref, wsm_ref, el_ref, rt_ref, v_out, ab_out,
     l3, r3, w3, gb, v3, t1, tq, t2, o3, sz, sy, rsb, xs, vs, u1, stage, rbuf, pbuf, obuf, obr, pin, dots, ra, rb, cg, gam, gram,
     rs_first, rs_last, rs_send, ag_first, ag_last, ag_send, fw_recv, fw_send, ra_recv, ra_send, rb_recv, rb_send,
-    st_sem, el_sem, rr_first, rr_last, rr_send, rf_recv, rf_send, ps_recv, ps_send, in_sem, ex_send, ex_recv,
+    st_sem, el_sem, rr_deep, rr_high, rr_low, rr_up, rr_send, rf_recv, rf_send, ps_recv, ps_send, in_sem, ex_send, ex_recv,
 ):
     z, yb, ya, x, core = (lax.axis_index(name) for name in AXES)
     row = lax.rem(ya + yb, 2)
@@ -112,7 +112,7 @@
     partner = a_peer(0, True)
     a_peers = [a_peer(d) for d in range(1, 8)] + [a_peer(d, True) for d in range(8)]
     b_peers = [b_peer(d) for d in range(1, 8)]
-    x_peers, ya_peer = a_peers[:3], a_peers[3]
+    x_peers, ya_peer = [a_peers[1], a_peers[0], a_peers[2]], a_peers[3]
     z_peers, yb_peer = b_peers[:3], b_peers[3]
 
     def rt_copy(p):
@@ -298,15 +298,14 @@
     def spare(i, slot):
         return rbuf.at[i // 2, lax.rem(i, 2), slot, :, top(LANE)]
 
-    def export_pack(vec):
-        for n in TRIO:
-            for sp in BOTH:
-                rows = [vec[2 * n + h, :, seg(sp, LANE)] for h in BOTH] + [jnp.zeros((32, LANE), F32)]
-                tile = jnp.concatenate(rows, axis=0).T
-                for s in BOTH:
-                    for g in range(8):
-                        to, off = divmod(8 * n + g, 3)
-                        obuf[to, seg(6 * sp + 3 * s + off, 8), :] = tile[seg(8 * s + g, 8), :]
+    def export_pack(vec, n):
+        for sp in BOTH:
+            rows = [vec[2 * n + h, :, seg(sp, LANE)] for h in BOTH] + [jnp.zeros((32, LANE), F32)]
+            tile = jnp.concatenate(rows, axis=0).T
+            for s in BOTH:
+                for g in range(8):
+                    to, off = divmod(8 * n + g, 3)
+                    obuf[to, seg(6 * sp + 3 * s + off, 8), :] = tile[seg(8 * s + g, 8), :]
 
     def export_send(i):
         for d, peer in enumerate(a_peers[:7]):
@@ -401,24 +400,29 @@
                     sy[k, i, j, :, seg(sp, LANE)] = val[PART:]
         rs_start(lax.rem(m, 2), k)
 
+    high, deep = top(40), pl.ds(40, 56)
+
+    def rg_send(c, who, rows, recv, peers):
+        part = rbuf.at[c, core, who, rows]
+        for peer in peers:
+            remote(part, part, rr_send.at[c], recv.at[c], peer)
+
+    def rg_wait(n, rows, sem):
+        wait_bytes(rbuf.at[0, 0, top(n), top(rows)], sem)
+
     def rg_start(c):
-        up, low = rbuf.at[c, core, mem, top(HALF)], rbuf.at[c, core, mem, pl.ds(HALF, HALF)]
-        for peer in x_peers:
-            remote(low, low, rr_send.at[c], rr_first.at[c], peer)
-        remote(up, up, rr_send.at[c], rr_first.at[c], ya_peer)
-        for peer in x_peers:
-            remote(up, up, rr_send.at[c], rr_last.at[c], peer)
+        rg_send(c, mem, deep, rr_deep, x_peers)
+        rg_send(c, mem, high, rr_high, [ya_peer])
+        rg_send(c, mem, high, rr_up, x_peers)
 
     def rg_bytes(n):
         return rbuf.at[0, 0, top(n)]
 
     def rg_second(c):
-        wait_bytes(rg_bytes(2), rr_first.at[c])
-        low = rbuf.at[c, core, pl.ds(ya * 4, 4), pl.ds(HALF, HALF)]
-        remote(low, low, rr_send.at[c], rr_last.at[c], ya_peer)
-        up = rbuf.at[c, core, (1 - ya) * 4 + x, top(HALF)]
-        for peer in x_peers:
-            remote(up, up, rr_send.at[c], rr_last.at[c], peer)
+        rg_wait(7, PART, rr_deep.at[c])
+        rg_wait(1, 40, rr_high.at[c])
+        rg_send(c, pl.ds(ya * 4, 4), deep, rr_low, [ya_peer])
+        rg_send(c, (1 - ya) * 4 + x, high, rr_up, x_peers)
 
     def rg_split(c):
         def piece(i):
@@ -442,7 +446,8 @@
         loop(8, piece)
 
     def rg_forward(c):
-        wait_bytes(rg_bytes(5), rr_last.at[c])
+        rg_wait(7, 32, rr_low.at[c])
+        rg_wait(5, HALF, rr_up.at[c])
         part = rbuf.at[c, core]
         remote(part, part, rf_send.at[c], rf_recv.at[c], partner)
 
@@ -612,16 +617,18 @@
                 wait_bytes(rbuf.at[0, 0], rf_send.at[c])
 
         spread(0)
+        pl.when(later)(export_done)
         rs_second(par, 4)
+        export_pack(vs.at[m], 0)
+        export_pack(vs.at[m], 1)
         advance(2)
         spread(1)
+        export_pack(vs.at[m], 2)
         advance(3)
         pl.when(more)(lambda: ag_forward(nxt, 0, 1))
         rs_second(par, 5)
         spread(2)
         advance(4)
-        pl.when(later)(export_done)
-        export_pack(vs.at[m])
 
     loop(STEPS, step)
 
@@ -631,7 +638,8 @@
     red_mid(0)
     red1_end(STEPS)
     export_done()
-    export_pack(u1)
+    for n in TRIO:
+        export_pack(u1, n)
     export_send(STEPS)
     red_mid(1)
     red2_end(STEPS, True)
@@ -683,7 +691,7 @@
             pltpu.VMEM((8, LANE), F32),
             pltpu.VMEM((STEPS, 8, LANE), F32),
             both, both, six, both, both, six, both, six, pair, pair, pair, pair,
-            dma((4,)), six, three, three, three, three, three, dma, dma, dma, dma, six,
+            dma((4,)), six, three, three, three, three, three, three, three, dma, dma, dma, dma, six,
         ],
         compiler_params=pltpu.CompilerParams(collective_id=0, has_side_effects=True, vmem_limit_bytes=67043328),
         name="lanczos",

time: 317 us -> 317 us (level)
  no operation moved by 1% of the time
where the time goes in v9:
time: 317 us; the launch traced here: 316 us
  Pallas kernels  311 us (98%)
  local copies, waits for them, and re-layouts  4.61 us (1%)
    pallas_call x1, Pallas kernels, run_kernel(): pl.pallas_call(kernel, out_shape=(jax.ShapeDtypeStruct((96, MROWS), F32),...  311 us

profile of v9, /device:TPU:1, one launch (start us, length us, event | category | flops | bytes accessed | tf_op | source)
XLA Modules:
  0.0 316.2 jit_solution(12752117115231236668)
XLA Ops:
  0.6 0.9 copy.7
  1.6 0.7 reshape.23.wsm_ref
  2.3 311.0 %lanczos.1 = (f32[96,768]{1,0:T(8,128)}, f32[8,128]{1,0:T(8,128)}) custom-call(f32[96,768]{1,0:T(8,128)} %bitcast.14, f32[32,32]{1,0:T(8,128)} %reshape.23.wsm_ref, f32[128,48,1536]{2,1,0:T(8,128)} %bitcast.13, f32[24,8,1536]{2,1,0:T(8,128)} %rt_ref.1), custom_call_target="tpu_custom_call" | custom-call | tf_op jit(solution)/shard_map/lanczos/pallas_call | solution.py:660
  313.3 1.3 slice_bitcast_fusion
  314.5 1.7 copy.9

commit v10 on v9

--- a/solution.py
+++ b/solution.py
@@ -12,6 +12,7 @@
 STEPS = 5
 AXES = ("z", "yb", "ya", "x", "core")
 F32, BF16 = jnp.float32, jnp.bfloat16
+ROWSUM = dict(axis=0, keepdims=True)
 MESH = pl.DeviceIdType.MESH
 D = 1536
 HALF = 48
@@ -48,7 +49,7 @@
     return dot(a[...], b[...]) + dot(a[:, : 2 * k], b[k:, :]) + dot(a[:, :k], b[2 * k :, :])
 
 
-BOTH, TRIO, QUAD = range(2), range(3), range(4)
+BOTH, TRIO, QUAD, EIGHT, SEVEN = range(2), range(3), range(4), range(8), range(1, 8)
 
 
 def loop(n, body):
@@ -110,8 +111,8 @@
         return {"z": lax.rem(z + d % 4, 4), "yb": to_yb, "ya": lax.rem(row + to_yb, 2), "x": x, "core": core}
 
     partner = a_peer(0, True)
-    a_peers = [a_peer(d) for d in range(1, 8)] + [a_peer(d, True) for d in range(8)]
-    b_peers = [b_peer(d) for d in range(1, 8)]
+    a_peers = [a_peer(d) for d in SEVEN] + [a_peer(d, True) for d in EIGHT]
+    b_peers = [b_peer(d) for d in SEVEN]
     x_peers, ya_peer = [a_peers[1], a_peers[0], a_peers[2]], a_peers[3]
     z_peers, yb_peer = b_peers[:3], b_peers[3]
 
@@ -130,7 +131,7 @@
 
     barrier = pltpu.get_barrier_semaphore()
     for peer in a_peers + b_peers:
-        pl.semaphore_signal(barrier, inc=1, device_id=peer, device_id_type=MESH)
+        pl.semaphore_signal(barrier, device_id=peer, device_id_type=MESH)
 
     def init(k):
         for i in range(STEPS):
@@ -151,7 +152,7 @@
         w3[:, seg(part, WIDE)] = jnp.where(same, full, 0.0).astype(BF16)
 
     psi_copy.wait()
-    for j in range(8):
+    for j in EIGHT:
         obr[j] = jnp.concatenate([pin[:, seg(8 * h + j, HALF)] for h in BOTH], axis=1)
     pl.semaphore_wait(barrier, len(a_peers) + len(b_peers))
 
@@ -243,7 +244,7 @@
     def red_rows(which, pairs):
         ra[which, ia] = jnp.zeros((16, LANE), F32)
         for src, dst in pairs:
-            ra[which, ia, row1(dst), :] = jnp.sum(dots[src], axis=0, keepdims=True)
+            ra[which, ia, row1(dst), :] = jnp.sum(dots[src], **ROWSUM)
         mine = ra.at[which, ia]
         for peer in a_peers:
             remote(mine, mine, ra_send.at[which], ra_recv.at[which], peer)
@@ -264,7 +265,7 @@
         wait_bytes(rb.at[which, top(7)], rb_recv.at[which])
         wait_bytes(rb.at[which, top(7)], rb_send.at[which])
         total = rb[which, 0]
-        for i in range(1, 8):
+        for i in SEVEN:
             total = total + rb[which, i]
         return jnp.broadcast_to(jnp.sum(total, axis=1, keepdims=True), (16, LANE))
 
@@ -281,7 +282,7 @@
         cg[...] = c8
         gram[jnp.maximum(m - 1, 0)] = total[8:]
         now = lax.broadcasted_iota(jnp.int32, c8.shape, 0) == m - 1
-        record(0, m, jnp.sum(jnp.where(now, c8, 0.0), axis=0, keepdims=True))
+        record(0, m, jnp.sum(jnp.where(now, c8, 0.0), **ROWSUM))
 
         def piece(k):
             cur = xs[m, k]
@@ -303,7 +304,7 @@
             rows = [vec[2 * n + h, :, seg(sp, LANE)] for h in BOTH] + [jnp.zeros((32, LANE), F32)]
             tile = jnp.concatenate(rows, axis=0).T
             for s in BOTH:
-                for g in range(8):
+                for g in EIGHT:
                     to, off = divmod(8 * n + g, 3)
                     obuf[to, seg(6 * sp + 3 * s + off, 8), :] = tile[seg(8 * s + g, 8), :]
 
@@ -323,7 +324,7 @@
         sq = total[8:9]
         for i in range(STEPS):
             di = d8[row1(i)]
-            inner = jnp.sum(d8 * gram[i], axis=0, keepdims=True)
+            inner = jnp.sum(d8 * gram[i], **ROWSUM)
             sq = sq - 2.0 * di * di + di * (2.0 * inner - di * gram[i, row1(i), :])
         beta = jnp.sqrt(sq)
         inv = 1.0 / beta
@@ -344,7 +345,7 @@
             export_done()
             loop(8, final)
             for h in BOTH:
-                v_out[:, seg(h, 384)] = jnp.concatenate([obuf[j, :, seg(h, HALF)] for j in range(8)], axis=1)
+                v_out[:, seg(h, 384)] = jnp.concatenate([obuf[j, :, seg(h, HALF)] for j in EIGHT], axis=1)
         else:
 
             def piece(k):
@@ -468,7 +469,7 @@
 
     wait_bytes(pbuf.at[top(7)], ps_recv)
     wait_bytes(pbuf.at[top(7)], ps_send)
-    for i in range(8):
+    for i in EIGHT:
         for s in QUAD:
             t1[seg(8 * s + i, PART), :96] = pbuf[i, seg(s, PART), :]
     for n in TRIO:

time: 317 us -> 317 us (level)
  no operation moved by 1% of the time
where the time goes in v10:
time: 317 us; the launch traced here: 316 us
  Pallas kernels  311 us (98%)
  local copies, waits for them, and re-layouts  4.61 us (1%)
    pallas_call x1, Pallas kernels, run_kernel(): pl.pallas_call(kernel, out_shape=(jax.ShapeDtypeStruct((96, MROWS), F32),...  311 us

profile of v10, /device:TPU:1, one launch (start us, length us, event | category | flops | bytes accessed | tf_op | source)
XLA Modules:
  0.0 316.2 jit_solution(12752117115231236668)
XLA Ops:
  0.6 0.9 copy.7
  1.6 0.7 reshape.23.wsm_ref
  2.3 311.0 %lanczos.1 = (f32[96,768]{1,0:T(8,128)}, f32[8,128]{1,0:T(8,128)}) custom-call(f32[96,768]{1,0:T(8,128)} %bitcast.14, f32[32,32]{1,0:T(8,128)} %reshape.23.wsm_ref, f32[128,48,1536]{2,1,0:T(8,128)} %bitcast.13, f32[24,8,1536]{2,1,0:T(8,128)} %rt_ref.1), custom_call_target="tpu_custom_call" | custom-call | tf_op jit(solution)/shard_map/lanczos/pallas_call | solution.py:661
  313.3 1.3 slice_bitcast_fusion
  314.5 1.7 copy.9

commit v11 on v10

--- a/solution.py
+++ b/solution.py
@@ -146,9 +146,13 @@
     i1 = lax.broadcasted_iota(jnp.int32, (WIDE, WIDE), 1)
     same = (i0 & 7) == ((i1 >> 3) & 7)
     left = ((i0 >> 3) == i1)[:, :32].astype(BF16)
-    right = (((i1 >> 6) * 8 + (i1 & 7)) == i0)[:32].astype(BF16)
-    for part, val in enumerate(split3(wsm_ref[...])):
-        full = dot(dot(left, val).astype(BF16), right)
+    col = lax.broadcasted_iota(jnp.int32, (LANE, 4 * WIDE), 1)
+    line = ((col & 7) << 4) + (((col >> 6) & 3) << 2) + (col >> 8)
+    pick = (line == lax.broadcasted_iota(jnp.int32, (LANE, 4 * WIDE), 0)).astype(BF16)
+    for part, val in enumerate(split3(wsm_ref[...].T)):
+        rows = dot(val, pick)
+        rows = jnp.concatenate([rows[:, seg(t, WIDE)] for t in QUAD], axis=0)
+        full = dot(left, rows.astype(BF16))
         w3[:, seg(part, WIDE)] = jnp.where(same, full, 0.0).astype(BF16)
 
     psi_copy.wait()
@@ -705,7 +709,7 @@
 
     def local_fn(psi_loc, env_left, env_right, mpo_pair):
         psi = jnp.transpose(psi_loc, (1, 2, 3, 0)).reshape(96, MROWS)
-        wsm = jnp.transpose(mpo_pair.reshape(8, 8, 4, 4), (3, 1, 2, 0)).reshape(32, 32)
+        wsm = jnp.moveaxis(mpo_pair, 1, -1).reshape(LANE, 8)
         vec, ab = run_kernel(psi, wsm, env_left.reshape(LANE, HALF, D), env_right)
         out = jnp.transpose(vec.reshape(2, 2, PART, MROWS), (3, 0, 1, 2))
         return ab[0, :STEPS], ab[1, :STEPS], out

time: 317 us -> 315 us (level)
  no operation moved by 1% of the time
where the time goes in v11:
time: 315 us
  Pallas kernels  311 us (99%)
    pallas_call x1, Pallas kernels, run_kernel(): pl.pallas_call(kernel, out_shape=(jax.ShapeDtypeStruct((96, MROWS), F32),...  311 us

profile of v11, /device:TPU:1, one launch (start us, length us, event | category | flops | bytes accessed | tf_op | source)
XLA Modules:
  0.0 314.8 jit_solution(14535803223853979527)
XLA Ops:
  0.6 311.1 %lanczos.1 = (f32[96,768]{1,0:T(8,128)}, f32[8,128]{1,0:T(8,128)}) custom-call(f32[96,768]{1,0:T(8,128)} %bitcast.16, f32[128,8]{1,0:T(8,128)} %bitcast.17, f32[128,48,1536]{2,1,0:T(8,128)} %bitcast.14, f32[24,8,1536]{2,1,0:T(8,128)} %rt_ref.1), custom_call_target="tpu_custom_call" | custom-call | tf_op jit(solution)/shard_map/lanczos/pallas_call | solution.py:665
  311.8 1.3 slice_bitcast_fusion
  313.1 1.7 copy.8

commit v12 on v11

--- a/solution.py
+++ b/solution.py
@@ -232,18 +232,24 @@
         up = sz[k, z, yb] + rsb[prev, k, 10]
         low = sy[k, yb, z] + rsb[prev, k, 11] + rsb[prev, k, 12] + rsb[prev, k, 13]
         w = jnp.concatenate([up, low], axis=0)
-        for i in range(STEPS):
-            w = w - wide(gam[row1(i), :]) * xs[i + 1, k]
+
+        def take(i, w):
+            return w - wide(gam[pl.ds(i, 1), :]) * xs[i + 1, k]
+
+        w = lax.fori_loop(0, m - 1, take, w)
         w = w * wide(gam[row1(STEPS), :])
         xs[m, k] = w
         local_dots(m, k, w)
 
     def local_dots(m, k, cur):
         new = vs[jnp.maximum(m - 1, 0), k]
-        for i in range(STEPS):
+
+        def one(i):
             vec = vs[i, k]
             dots[i] = dots[i] + fold(vec * cur)
             dots[STEPS + i] = dots[STEPS + i] + fold(vec * new)
+
+        loop(m, one)
 
     def red_rows(which, pairs):
         ra[which, ia] = jnp.zeros((16, LANE), F32)

time: 315 us -> 315 us (level)
  no operation moved by 1% of the time
where the time goes in v12:
time: 315 us
  Pallas kernels  311 us (99%)
    pallas_call x1, Pallas kernels, run_kernel(): pl.pallas_call(kernel, out_shape=(jax.ShapeDtypeStruct((96, MROWS), F32),...  311 us

profile of v12, /device:TPU:1, one launch (start us, length us, event | category | flops | bytes accessed | tf_op | source)
XLA Modules:
  0.0 314.5 jit_solution(3775480851536360546)
XLA Ops:
  0.6 310.9 %lanczos.1 = (f32[96,768]{1,0:T(8,128)}, f32[8,128]{1,0:T(8,128)}) custom-call(f32[96,768]{1,0:T(8,128)} %bitcast.16, f32[128,8]{1,0:T(8,128)} %bitcast.17, f32[128,48,1536]{2,1,0:T(8,128)} %bitcast.14, f32[24,8,1536]{2,1,0:T(8,128)} %rt_ref.1), custom_call_target="tpu_custom_call" | custom-call | tf_op jit(solution)/shard_map/lanczos/pallas_call | solution.py:671
  311.6 1.3 slice_bitcast_fusion
  312.8 1.7 copy.8
